TPU v7x, 8 devices: a whole 2x2x1 slice. The times are simulated.
8 devices in a mesh: mp: 2 (over z, y), fsdp: 4 (over x, core).
Axes of the slice: x: 2, y: 2, z: 1, core: 2. Of those that a mesh axis runs over, the one named last changes fastest.
Arguments:
- x: bfloat16 [1, 8, 4096, 1536], P(None, ('mp', 'fsdp')), parts along dimension 1
- dy: bfloat16 [8, 4096, 1536], P(('mp', 'fsdp')), parts along dimension 0
- xn: bfloat16 [8, 4096, 1536], P(('mp', 'fsdp')), parts along dimension 0
- w1: float32 [1, 3072, 6144], P(None, ('mp', 'fsdp')), parts along dimension 1
- w2: float32 [1, 12288, 1536], P(None, ('mp', 'fsdp')), parts along dimension 1
- g1: float32 [1, 3072, 6144], P(None, ('mp', 'fsdp')), parts along dimension 1
- g2: float32 [1, 12288, 1536], P(None, ('mp', 'fsdp')), parts along dimension 1
- m1: float32 [1, 3072, 6144], P(None, ('mp', 'fsdp')), parts along dimension 1
- m2: float32 [1, 12288, 1536], P(None, ('mp', 'fsdp')), parts along dimension 1
- v1: float32 [1, 3072, 6144], P(None, ('mp', 'fsdp')), parts along dimension 1
- v2: float32 [1, 12288, 1536], P(None, ('mp', 'fsdp')), parts along dimension 1
- hp: float32 [5], replicated
- step: int32 [1], replicated
Outputs:
- output 1: float32 [1, 3072, 6144], P(None, ('mp', 'fsdp')), parts along dimension 1
- output 2: float32 [1, 12288, 1536], P(None, ('mp', 'fsdp')), parts along dimension 1
- output 3: float32 [1, 3072, 6144], P(None, ('mp', 'fsdp')), parts along dimension 1
- output 4: float32 [1, 12288, 1536], P(None, ('mp', 'fsdp')), parts along dimension 1
- output 5: float32 [1, 3072, 6144], P(None, ('mp', 'fsdp')), parts along dimension 1
- output 6: float32 [1, 12288, 1536], P(None, ('mp', 'fsdp')), parts along dimension 1
- output 7: bfloat16 [8, 4096, 1536], P(('mp', 'fsdp')), parts along dimension 0
There are 2 independent parts. A program takes and returns all parts, laid end to end along the dimension named above; an argument that names none is the same for every part.
All inputs are finite; a program needn't handle non-finite values.
Results may differ from a plain program's by a relative error of at most 0.00473703.
Values are sent between devices in bfloat16 or wider.
A program may use at most 1 GiB of HBM per device.

v0:
```python
import jax
import jax.numpy as jnp
from jax import lax
from jax.sharding import PartitionSpec as P


def gelu(h):
    return jax.nn.gelu(h, approximate=True)


def adam(w, ga, s, m, v, hp, tf):
    lr, b1, b2, eps, wd = hp[0], hp[1], hp[2], hp[3], hp[4]
    g = (ga + s) / 2.0
    mn = b1 * m + (1.0 - b1) * g
    vn = b2 * v + (1.0 - b2) * g * g
    upd = (mn / (1.0 - b1 ** tf)) / (jnp.sqrt(vn / (1.0 - b2 ** tf)) + eps)
    return w - lr * (upd + wd * w), mn, vn


def solution(mesh):
    n = mesh.shape['fsdp']
    f32 = jnp.float32
    bf = jnp.bfloat16
    tok4 = P(None, ('mp', 'fsdp'), None, None)
    tok3 = P(('mp', 'fsdp'), None, None)
    rows = P(None, ('mp', 'fsdp'), None)

    def gather(w):
        return lax.all_gather(w.astype(bf), 'fsdp', axis=0, tiled=True)

    def scatter_sum(p):
        q = lax.all_to_all(p, 'fsdp', 0, 0, tiled=True)
        return jnp.sum(q.reshape(n, p.shape[0] // n, p.shape[1]), axis=0, dtype=f32)

    def body(x, dy, xn, w1, w2, g1, g2, m1, m2, v1, v2, hp, step):
        nl, b, t, d = x.shape
        tf = step[0].astype(f32)
        gy = dy.reshape(b * t, d)
        res = [None] * nl
        for l in reversed(range(nl)):
            c1 = gather(w1[l])
            c2 = gather(w2[l])
            xl = x[l].reshape(b * t, d)
            h = jnp.dot(xl, c1, preferred_element_type=f32)
            a, gv = jax.vjp(gelu, h)
            a = a.astype(bf)
            da = jnp.einsum('nd,fd->nf', gy, c2, preferred_element_type=f32)
            dh = gv(da)[0].astype(bf)
            p2 = jnp.einsum('nf,nd->fd', a, gy, preferred_element_type=f32).astype(bf)
            p1 = jnp.einsum('nd,nf->df', xl, dh, preferred_element_type=f32).astype(bf)
            if l > 0:
                gy = (gy.astype(f32) + jnp.einsum('nf,df->nd', dh, c1, preferred_element_type=f32)).astype(bf)
            s1 = scatter_sum(p1)
            s2 = scatter_sum(p2)
            res[l] = (adam(w1[l], g1[l], s1, m1[l], v1[l], hp, tf),
                      adam(w2[l], g2[l], s2, m2[l], v2[l], hp, tf))
        xc = xn.reshape(b * t, d)
        for l in range(nl):
            c1 = gather(res[l][0][0])
            c2 = gather(res[l][1][0])
            h = jnp.dot(xc, c1, preferred_element_type=f32)
            a = gelu(h).astype(bf)
            xc = (xc.astype(f32) + jnp.dot(a, c2, preferred_element_type=f32)).astype(bf)

        def stack(i, j):
            return jnp.stack([res[l][i][j] for l in range(nl)])

        return (stack(0, 0), stack(1, 0), stack(0, 1), stack(1, 1), stack(0, 2), stack(1, 2),
                xc.reshape(b, t, d))

    return jax.shard_map(body, mesh=mesh,
                         in_specs=(tok4, tok3, tok3) + (rows,) * 8 + (P(), P()),
                         out_specs=(rows,) * 6 + (tok3,), check_vma=False)
```

profile of v0, /device:TPU:0, one launch (start us, length us, event | category | flops | bytes accessed | tf_op | source)
XLA Modules:
  0.0 1531.9 jit_solution(15245201690172311344)
XLA Ops:
  7.2 0.0 all-gather.7.cloned.1.call-start
  7.2 6.5 bitcast_convert_fusion
  13.8 0.0 all-gather.7.cloned.1.call-update
  13.8 121.0 %all-gather.7.cloned.1.call-done = bf16[1536,6144]{1,0:T(8,128)(2,1)} async-done(((bf16[384,6144]{1,0:T(8,128)(2,1)}), bf16[1536,6144]{1,0:T(8,128)(2,1)}) %all-gather.7.cloned.1.call-update) | async-done | bytes 18874384 | tf_op jit(solution)/shard_map/all_gather | solution.py:29
  134.8 88.6 %fusion.20 = f32[4096,6144]{1,0:T(8,128)} fusion(bf16[1536,6144]{1,0:T(8,128)(2,1)} %all-gather.7.cloned.1.call-done, bf16[1,1,4096,1536]{3,2,1,0:T(8,128)(2,1)} %param.13), kind=kOutput, calls=%fused_computation.28 | convolution fusion | flops 77309411328 | bytes 132120576 | tf_op jit(solution)/shard_map/dot_general | solution.py:44
  223.4 100.8 %fusion.16 = bf16[6144,1536]{1,0:T(8,128)(2,1)} fusion(f32[4096,6144]{1,0:T(8,128)} %fusion.20, bf16[1,4096,1536]{2,1,0:T(8,128)(2,1)} %param.14), kind=kOutput, calls=%fused_computation.23 | convolution fusion | flops 77545340928 | bytes 132120576 | tf_op jit(solution)/shard_map/nf,nd->fd/dot_general | solution.py:49
  324.1 0.0 copy-start
  324.1 7.5 all-to-all-start.1
  331.6 0.0 all-gather.5.cloned.1.call-start
  332.3 0.0 copy-done
  332.3 0.6 fusion.42
  335.7 201.1 %all-to-all-done.1 = bf16[4,1536,1536]{2,1,0:T(8,128)(2,1)} async-done(((bf16[4,1536,1536]{2,1,0:T(8,128)(2,1)}), bf16[4,1536,1536]{2,1,0:T(8,128)(2,1)}, u32[]{:S(2)}, u32[]{:S(2)}) %all-to-all-start.1) | async-done | bytes 18874400 | tf_op jit(solution)/shard_map/all_to_all | solution.py:32
  536.8 14.7 convert_reduce_fusion
  551.4 31.8 %multiply_subtract_fusion = (f32[1,1536,1536]{2,1,0:T(8,128)}, f32[1,1536,1536]{2,1,0:T(8,128)}, f32[1,1536,1536]{2,1,0:T(8,128)}, bf16[1536,1536]{1,0:T(8,128)(2,1)}) fusion(f32[1,1536,1536]{2,1,0:T(8,128)} %param.17, f32[]{:T(128)} %bitcast.12, f32[]{:T(128)} %bitcast.11, f32[]{:T(128)S(6)} %sub.35, f32[]{:T(128)S(6)} %sub.33, f32[]{:T(128)} %bitcast, ...), kind=kLoop, calls=%fused_computation.60 | loop fusion | flops 42467328 | bytes 80216096 | tf_op jit(solution)/shard_map/sub | solution.py:17
  583.2 0.0 all-gather.5.cloned.1.call-update
  583.3 0.0 all-gather.9.cloned.1.call-start
  583.3 118.2 %all-gather.5.cloned.1.call-done = bf16[6144,1536]{1,0:T(8,128)(2,1)} async-done(((bf16[1536,1536]{1,0:T(8,128)(2,1)}), bf16[6144,1536]{1,0:T(8,128)(2,1)}) %all-gather.5.cloned.1.call-update) | async-done | bytes 18874384 | tf_op jit(solution)/shard_map/all_gather | solution.py:29
  701.5 149.4 %fusion.6 = bf16[4096,6144]{1,0:T(8,128)(2,1)} fusion(f32[4096,6144]{1,0:T(8,128)} %fusion.20, bf16[6144,1536]{1,0:T(8,128)(2,1)} %all-gather.5.cloned.1.call-done, bf16[1,4096,1536]{2,1,0:T(8,128)(2,1)} %param.14), kind=kOutput, calls=%fused_computation.9 | convolution fusion | flops 77812727808 | bytes 182452224 | tf_op jit(solution)/shard_map/nd,fd->nf/dot_general | solution.py:47
  850.9 92.3 %convolution_convert_fusion = bf16[6144,1536]{0,1:T(8,128)(2,1)} fusion(bf16[4096,6144]{1,0:T(8,128)(2,1)} %fusion.6, bf16[1,1,4096,1536]{3,2,1,0:T(8,128)(2,1)} %param.13), kind=kOutput, calls=%fused_computation.24 | convolution fusion | flops 77318848512 | bytes 81788928 | tf_op jit(solution)/shard_map/nd,nf->df/dot_general | solution.py:50
  943.2 217.6 %all_to_all.18 = bf16[4,384,6144]{2,1,0:T(8,128)(2,1)} all-to-all(bf16[4,384,6144]{2,1,0:T(8,128)(2,1)} %bitcast.124), channel_id=1, replica_groups=mesh['mp'=2,'fsdp'=4] {'fsdp'}, dimensions={0} | all-to-all | bytes 37748736 | tf_op jit(solution)/shard_map/all_to_all | solution.py:32
  1160.8 14.8 convert_reduce_fusion.1
  1175.6 22.7 %fusion.36 = bf16[384,6144]{1,0:T(8,128)(2,1)} fusion(f32[1,384,6144]{2,1,0:T(8,128)} %param.16, f32[384,6144]{1,0:T(8,128)} %convert_reduce_fusion.1, f32[1,384,6144]{2,1,0:T(8,128)} %param.18, f32[1,384,6144]{2,1,0:T(8,128)} %param.22, f32[1,384,6144]{2,1,0:T(8,128)} %param.20, f32[]{:T(128)} %bitcast.12, f32[]{:T(128)} %bitcast.11, f32[]{:T(128)S(6)} %sub.35, ...), kind=kLoop, calls=%fused_computation.55 | loop fusion | flops 42467328 | bytes 51904548 | tf_op jit(solution)/shard_map/convert_element_type | solution.py:29
  1198.2 0.0 all-gather.9.cloned.1.call-update
  1198.3 0.0 all-gather.11.cloned.1.call-start
  1198.3 22.7 %fusion.37 = bf16[1536,1536]{1,0:T(8,128)(2,1)} fusion(f32[1,1536,1536]{2,1,0:T(8,128)} %param.17, f32[1536,1536]{1,0:T(8,128)} %convert_reduce_fusion, f32[1,1536,1536]{2,1,0:T(8,128)} %param.19, f32[1,1536,1536]{2,1,0:T(8,128)} %param.23, f32[1,1536,1536]{2,1,0:T(8,128)} %param.21, f32[]{:T(128)} %bitcast.12, f32[]{:T(128)} %bitcast.11, f32[]{:T(128)S(6)} %sub.35, ...), kind=kLoop, calls=%fused_computation.59 | loop fusion | flops 42467328 | bytes 51904548 | tf_op jit(solution)/shard_map/convert_element_type | solution.py:29
  1221.0 0.0 all-gather.11.cloned.1.call-update
  1221.0 30.4 %multiply_subtract_fusion.1 = (f32[1,384,6144]{2,1,0:T(8,128)}, f32[1,384,6144]{2,1,0:T(8,128)}, f32[1,384,6144]{2,1,0:T(8,128)}) fusion(f32[1,384,6144]{2,1,0:T(8,128)} %param.16, f32[]{:T(128)} %bitcast.12, f32[]{:T(128)} %bitcast.11, f32[]{:T(128)S(6)} %sub.35, f32[]{:T(128)S(6)} %sub.33, f32[]{:T(128)} %bitcast, f32[]{:T(128)S(6)} %mul.232, ...), kind=kLoop, calls=%fused_computation.63 | loop fusion | flops 40108032 | bytes 75497504 | tf_op jit(solution)/shard_map/sub | solution.py:17
  1251.4 65.1 %all-gather.9.cloned.1.call-done = bf16[1536,6144]{1,0:T(8,128)(2,1)} async-done(((bf16[384,6144]{1,0:T(8,128)(2,1)}), bf16[1536,6144]{1,0:T(8,128)(2,1)}) %all-gather.9.cloned.1.call-update) | async-done | bytes 18874384 | tf_op jit(solution)/shard_map/all_gather | solution.py:29
  1316.5 108.2 %fusion.14 = bf16[4096,6144]{1,0:T(8,128)(2,1)} fusion(bf16[1536,6144]{1,0:T(8,128)(2,1)} %all-gather.9.cloned.1.call-done, bf16[1,4096,1536]{2,1,0:T(8,128)(2,1)} %param.15), kind=kOutput, calls=%fused_computation.17 | convolution fusion | flops 77535903744 | bytes 81788928 | tf_op jit(solution)/shard_map/dot_general | solution.py:61
  1424.6 11.3 all-gather.11.cloned.1.call-done
  1436.0 89.2 %fusion.17 = bf16[1,4096,1536]{2,1,0:T(8,128)(2,1)} fusion(bf16[4096,6144]{1,0:T(8,128)(2,1)} %fusion.14, bf16[6144,1536]{1,0:T(8,128)(2,1)} %all-gather.11.cloned.1.call-done, bf16[1,4096,1536]{2,1,0:T(8,128)(2,1)} %param.15), kind=kOutput, calls=%fused_computation.25 | convolution fusion | flops 77328285696 | bytes 94371840 | tf_op jit(solution)/shard_map/dot_general | solution.py:63
Async XLA Ops:
  7.2 127.7 %all-gather.7.cloned.1.call-start = ((), (), s32[]{:S(2)}) async-start(), calls=%async_computation.3 | async-start | bytes 23592960 | tf_op jit(solution)/shard_map/all_gather | solution.py:29
  324.1 8.2 copy-start
  324.1 212.7 %all-to-all-start.1 = ((bf16[4,1536,1536]{2,1,0:T(8,128)(2,1)}), bf16[4,1536,1536]{2,1,0:T(8,128)(2,1)}, u32[]{:S(2)}, u32[]{:S(2)}) async-start(bf16[4,1536,1536]{2,1,0:T(8,128)(2,1)} %bitcast.123), calls=%async_computation.1 | async-start | bytes 37748736 | tf_op jit(solution)/shard_map/all_to_all | solution.py:32
  331.6 369.9 %all-gather.5.cloned.1.call-start = ((), (), s32[]{:S(2)}) async-start(), calls=%async_computation.2 | async-start | bytes 23592960 | tf_op jit(solution)/shard_map/all_gather | solution.py:29
  583.3 733.2 %all-gather.9.cloned.1.call-start = ((), (), s32[]{:S(2)}) async-start(), calls=%async_computation.4 | async-start | bytes 23592960 | tf_op jit(solution)/shard_map/all_gather | solution.py:29
  1198.3 237.7 %all-gather.11.cloned.1.call-start = ((), (), s32[]{:S(2)}) async-start(), calls=%async_computation.5 | async-start | bytes 23592960 | tf_op jit(solution)/shard_map/all_gather | solution.py:29
Sparse Core Ops, SparseCore 0:
  13.9 120.8 all-gather.6
  583.4 118.0 all-gather.4
  1198.4 118.0 all-gather.8
  1317.9 118.0 all-gather.10
where the time goes:
time: 1540 us; the launch traced here: 1530 us
  matrix products  628 us (41%)
  waiting for transfers between devices  517 us (34%)
  blocking collectives  218 us (14%)
  other arithmetic  144 us (9%)
  between operations  17.3 us (1%)
    all_gather x4, waiting for transfers between devices, gather(): return lax.all_gather(w.astype(bf), 'fsdp', axis=0, tiled=True)  316 us
    all_to_all x1, blocking collectives, scatter_sum(): q = lax.all_to_all(p, 'fsdp', 0, 0, tiled=True)  218 us
    all_to_all x1, waiting for transfers between devices, scatter_sum(): q = lax.all_to_all(p, 'fsdp', 0, 0, tiled=True)  201 us
    dot_general x1, matrix products, body(): da = jnp.einsum('nd,fd->nf', gy, c2, preferred_element_type=f32)  149 us
    dot_general x1, matrix products, body(): h = jnp.dot(xc, c1, preferred_element_type=f32)  108 us
    dot_general x1, matrix products, body(): p2 = jnp.einsum('nf,nd->fd', a, gy, preferred_element_type=f32).astype(bf)  101 us
    dot_general x1, matrix products, body(): p1 = jnp.einsum('nd,nf->df', xl, dh, preferred_element_type=f32).astype(bf)  92.3 us
    dot_general x1, matrix products, body(): jnp.dot(a, c2, preferred_element_type=f32)  89.2 us
  transfers between devices with their start and end apart: 5, of which 5 were waited for; matrix products, arithmetic and copies ran while one was open for 11% of the time, Pallas kernels for 0%

commit v1 on v0

v1 whole, which is shorter than its diff:
```python
import functools

import jax
import jax.numpy as jnp
from jax import lax
from jax.experimental import pallas as pl
from jax.experimental.pallas import tpu as pltpu
from jax.sharding import PartitionSpec as P


NK = 4
TM = 512
TN = 512
C0 = 0.7978845608028654
C1 = 0.044715
f32 = jnp.float32
bf = jnp.bfloat16
VMEM = 60 * 1024 * 1024
LATER = pl.BlockSpec(memory_space=pl.ANY)


def params(n=1):
    return pltpu.CompilerParams(vmem_limit_bytes=VMEM, dimension_semantics=("arbitrary",) * n)


def whole(shape, row=0):
    return pl.BlockSpec(shape, lambda *_: (row, 0), pipeline_mode=pl.Buffered(1))


def cost(flops, nbytes):
    return pl.CostEstimate(flops=flops, bytes_accessed=nbytes, transcendentals=0)


def cast_kernel(w1, w2, out):
    r = w1.shape[0]
    out[:r] = w1[...].astype(bf)
    out[r:] = w2[...].astype(bf)


def cast_chunk(w1, w2, k, n):
    r, cb = w1.shape[0], w1.shape[1] // (n * NK)
    d = w2.shape[1]
    rb, dc = w2.shape[0] // NK, d // n
    return pl.pallas_call(
        cast_kernel, grid=(n,),
        in_specs=[pl.BlockSpec((r, cb), lambda j: (0, j * NK + k)),
                  pl.BlockSpec((rb, dc), lambda j: (k, j))],
        out_specs=pl.BlockSpec((r + rb, cb), lambda j: (0, j)),
        out_shape=jax.ShapeDtypeStruct((r + rb, d), bf),
        cost_estimate=cost(r * d * 2, r * d * 12),
        name="cast_chunk", compiler_params=params())(w1, w2)


def join1(me, cs, n, w1):
    b = cs[0].shape[0]
    w = w1.shape[1] // n
    for q in range(n):
        for r in range(n):
            j = pl.multiple_of((me ^ r) * w, 128)
            w1[pl.ds(pl.multiple_of((me ^ q) * b, 128), b), r * w:(r + 1) * w] = cs[q][:, pl.ds(j, w)]


def join2(cs, n, w2):
    b = cs[0].shape[0]
    for q in range(n):
        w2[q * b:(q + 1) * b, :] = cs[q][...]


def hid_kernel(n, me, x, dy, *refs):
    c1, c2 = refs[:n], refs[n:2 * n]
    a_out, dh_out, w1, w2 = refs[-4:]

    @pl.when(pl.program_id(0) == 0)
    def _():
        join1(me[0], c1, n, w1)
        join2(c2, n, w2)

    xv = x[...]
    dv = dy[...]
    for s in range(0, w1.shape[1], TN):
        h = jnp.dot(xv, w1[:, s:s + TN], preferred_element_type=f32)
        da = lax.dot_general(dv, w2[s:s + TN, :], (((1,), (1,)), ((), ())),
                             preferred_element_type=f32)
        hh = h * h
        t = jnp.tanh(h * (C0 + (C0 * C1) * hh))
        p = 0.5 + 0.5 * t
        a_out[:, s:s + TN] = (h * p).astype(bf)
        gp = p + (0.5 * h) * (1.0 - t * t) * (C0 + (3.0 * C0 * C1) * hh)
        dh_out[:, s:s + TN] = (da * gp).astype(bf)


def hid(me, x, dy, cs, after):
    n = len(cs)
    t, d = x.shape
    h2, w = cs[0].shape
    hh = h2 // 2
    tok = pl.BlockSpec((TM, d), lambda i, *_: (i, 0))
    return pl.pallas_call(
        functools.partial(hid_kernel, n),
        grid_spec=pltpu.PrefetchScalarGridSpec(
            num_scalar_prefetch=1, grid=(t // TM,),
            in_specs=[tok, tok] + [whole((hh, w))] * n + [whole((hh, w), 1)] * n + [LATER] * len(after),
            out_specs=[pl.BlockSpec((TM, w), lambda i, *_: (i, 0))] * 2,
            scratch_shapes=[pltpu.VMEM((n * hh, w), bf), pltpu.VMEM((n * hh, d), bf)]),
        out_shape=[jax.ShapeDtypeStruct((t, w), bf)] * 2,
        cost_estimate=cost(4 * t * d * w, 8 * t * d),
        name="hid", compiler_params=params())(me, x, dy, *cs, *cs, *after)


def up_kernel(n, me, x, *refs):
    c1 = refs[:n]
    a_out, w1 = refs[-2:]

    @pl.when(pl.program_id(0) == 0)
    def _():
        join1(me[0], c1, n, w1)

    xv = x[...]
    for s in range(0, w1.shape[1], TN):
        h = jnp.dot(xv, w1[:, s:s + TN], preferred_element_type=f32)
        t = jnp.tanh(h * (C0 + (C0 * C1) * (h * h)))
        a_out[:, s:s + TN] = (h * (0.5 + 0.5 * t)).astype(bf)


def up(me, x, cs, after):
    n = len(cs)
    t, d = x.shape
    h2, w = cs[0].shape
    hh = h2 // 2
    return pl.pallas_call(
        functools.partial(up_kernel, n),
        grid_spec=pltpu.PrefetchScalarGridSpec(
            num_scalar_prefetch=1, grid=(t // TM,),
            in_specs=[pl.BlockSpec((TM, d), lambda i, *_: (i, 0))] + [whole((hh, w))] * n
            + [LATER] * len(after),
            out_specs=pl.BlockSpec((TM, w), lambda i, *_: (i, 0)),
            scratch_shapes=[pltpu.VMEM((n * hh, w), bf)]),
        out_shape=jax.ShapeDtypeStruct((t, w), bf),
        cost_estimate=cost(2 * t * d * w, 4 * t * d),
        name="up", compiler_params=params())(me, x, *cs, *after)


def down_kernel(n, a, acc, *refs):
    c2 = refs[:n]
    out, w2 = refs[n:]

    @pl.when(pl.program_id(0) == 0)
    def _():
        join2(c2, n, w2)

    av = a[...]
    for s in range(0, w2.shape[1], TN):
        o = jnp.dot(av, w2[:, s:s + TN], preferred_element_type=f32)
        out[:, s:s + TN] = (acc[:, s:s + TN].astype(f32) + o).astype(out.dtype)


def down(a, acc, cs, dtype):
    n = len(cs)
    t, w = a.shape
    h2, d = cs[0].shape
    hh = h2 // 2
    tok = pl.BlockSpec((TM, d), lambda i: (i, 0))
    return pl.pallas_call(
        functools.partial(down_kernel, n), grid=(t // TM,),
        in_specs=[pl.BlockSpec((TM, w), lambda i: (i, 0)), tok] + [whole((hh, d), 1)] * n,
        out_specs=tok,
        scratch_shapes=[pltpu.VMEM((n * hh, d), bf)],
        out_shape=jax.ShapeDtypeStruct((t, d), dtype),
        cost_estimate=cost(2 * t * d * w, 10 * t * d),
        name="down", compiler_params=params())(a, acc, *cs)


def adam_kernel(n, me, sc, *refs):
    lr, b1, b2, eps, wd, u1, u2 = (sc[i] for i in range(7))
    p1, p2 = refs[:n], refs[n:2 * n]
    wi = refs[2 * n:2 * n + 8]
    outs = refs[-7:]
    b = outs[6].shape[0] // 2
    for half, ps in ((0, p1), (1, p2)):
        w, ga, m, v = (wi[half * 4 + i][...] for i in range(4))
        s = ps[0][...].astype(f32)
        for q in range(1, n):
            s = s + ps[q][...].astype(f32)
        g = (ga + s) / 2.0
        mn = b1 * m + (1.0 - b1) * g
        vn = b2 * v + (1.0 - b2) * g * g
        upd = (mn / u1) / (jnp.sqrt(vn / u2) + eps)
        wn = w - lr * (upd + wd * w)
        outs[half * 3][...] = wn
        outs[half * 3 + 1][...] = mn
        outs[half * 3 + 2][...] = vn
        outs[6][half * b:(half + 1) * b, :] = wn.astype(bf)


def adam(me, sc, p1, got1, p2, got2, st1, st2, prev, k, after):
    n = len(got1) + 1
    r, ff = st1[0].shape
    f, d = st2[0].shape
    cb, rb, dc = ff // (n * NK), f // NK, d // n

    def col(q):
        return pl.BlockSpec((r, cb), lambda j, me, sc: (0 if q else me[0], me[0] ^ q ^ j))

    def straight():
        return pl.BlockSpec((rb, dc), lambda j, me, sc: (0, j))

    s1 = pl.BlockSpec((r, cb), lambda j, me, sc: (0, j * NK + k))
    s2 = pl.BlockSpec((rb, dc), lambda j, me, sc: (k, j))
    specs = ([col(q) for q in range(n)] + [straight()] * n
             + [s1] * 4 + [s2] * 4)
    args = [p1] + got1 + [p2] + got2 + st1 + st2
    alias = {}
    if prev is not None:
        alias = {2 + len(args) + i: i for i in range(6)}
        specs = specs + [pl.BlockSpec(memory_space=pl.ANY)] * 6
        args = args + prev
    specs = specs + [LATER] * len(after)
    args = args + after
    out = pl.pallas_call(
        functools.partial(adam_kernel, n),
        grid_spec=pltpu.PrefetchScalarGridSpec(
            num_scalar_prefetch=2, grid=(n,), in_specs=specs,
            out_specs=[s1] * 3 + [s2] * 3 + [pl.BlockSpec((r + rb, cb), lambda j, me, sc: (0, j))]),
        out_shape=[jax.ShapeDtypeStruct((r, ff), f32)] * 3
        + [jax.ShapeDtypeStruct((f, d), f32)] * 3 + [jax.ShapeDtypeStruct((r + rb, d), bf)],
        input_output_aliases=alias,
        cost_estimate=cost(r * d * 60, r * d * 76),
        name="adam", compiler_params=params())(me, sc, *args)
    return list(out[:6]), out[6]


def solution(mesh):
    n = mesh.shape['fsdp']
    tok4 = P(None, ('mp', 'fsdp'), None, None)
    tok3 = P(('mp', 'fsdp'), None, None)
    rows = P(None, ('mp', 'fsdp'), None)

    def hop(a, r):
        return lax.ppermute(a, 'fsdp', [(i, i ^ r) for i in range(n)])

    def gather(c):
        far = hop(c, 2)
        own = hop(c, 1)
        near = hop(far, 1)
        return [c, own, far, near]

    def body(x, dy, xn, w1, w2, g1, g2, m1, m2, v1, v2, hp, step):
        _, b, t, d = x.shape
        ds = d // n
        tf = step[0].astype(f32)
        me = lax.axis_index('fsdp')
        mev = me.astype(jnp.int32).reshape(1)
        gy = dy.reshape(b * t, d)
        sc = jnp.stack([hp[0], hp[1], hp[2], hp[3], hp[4],
                        1.0 - hp[1] ** tf, 1.0 - hp[2] ** tf, hp[0]])

        xl = x.reshape(b * t, d)
        xc = xn.reshape(b * t, d)
        cs = [gather(cast_chunk(w1[0], w2[0], k, n))
              for k in range(NK)]
        st1 = [w1[0], g1[0], m1[0], v1[0]]
        st2 = [w2[0], g2[0], m2[0], v2[0]]
        parts = [None] * NK

        def back(k, after):
            a, dh = hid(mev, xl, gy, cs[k], after)
            p2 = jnp.einsum('nf,nd->fd', a, gy, preferred_element_type=f32).astype(bf)
            p1 = jnp.einsum('nd,nf->df', xl, dh, preferred_element_type=f32).astype(bf)
            s2 = [p2[r * ds:(r + 1) * ds] for r in range(1, n)]
            s1 = [lax.dynamic_slice_in_dim(p1, (me ^ r) * ds, ds, 0) for r in range(1, n)]
            r2 = [hop(q, r) for r, q in enumerate(s2, 1)]
            r1 = [hop(q, r) for r, q in enumerate(s1, 1)]
            parts[k] = p1, r1, p2, r2
            return s1 + s2

        def step_of(k, prev, after):
            prev, c = adam(mev, sc, *parts[k], st1, st2, prev, k, after)
            return prev, [c], gather(c)

        def ahead(k, full, acc, after):
            a = up(mev, xc, full, after)
            return down(a, acc, full, bf if k == NK - 1 else f32)

        full = [None] * NK
        later = back(0, [])
        later = back(1, later)
        later = back(2, later)
        prev, later, full[0] = step_of(0, None, later)
        prev, later, full[1] = step_of(1, prev, later)
        later = back(3, later)
        prev, later, full[2] = step_of(2, prev, later)
        acc = ahead(0, full[0], xc, later)
        acc = ahead(1, full[1], acc, [])
        prev, later, full[3] = step_of(3, prev, [acc])
        acc = ahead(2, full[2], acc, later)
        acc = ahead(3, full[3], acc, [acc])
        w1n, m1n, v1n, w2n, m2n, v2n = prev
        return (w1n[None], w2n[None], m1n[None], m2n[None], v1n[None], v2n[None],
                acc.reshape(b, t, d))

    return jax.shard_map(body, mesh=mesh,
                         in_specs=(tok4, tok3, tok3) + (rows,) * 8 + (P(), P()),
                         out_specs=(rows,) * 6 + (tok3,), check_vma=False)
```

time: 1540 us -> 1140 us (0.74)
  Pallas kernels: 0 us -> 510 us
  matrix products: 628 us -> 206 us
  blocking collectives: 218 us -> 0 us
  waiting for transfers between devices: 517 us -> 356 us
  other arithmetic: 144 us -> 1.3 us
  starting transfers between devices: 7.63 us -> 35 us
  local copies, waits for them, and re-layouts: 0.65 us -> 23.3 us
    pallas_call x0 -> x20, Pallas kernels: none -> 510 us  [the longest x4 199 us: hid(): pl.pallas_call(functools.partial(hid_kernel, n), grid_spec=pltpu.Prefetch...]
    dot_general x6 -> x8, matrix products: 628 us -> 206 us  [the longest x4 105 us: back(): p1 = jnp.einsum('nd,nf->df', xl, dh, preferred_element_type=f32).astype(bf)]
    ppermute x0 -> x48, waiting for transfers between devices: none -> 356 us  [hop(): return lax.ppermute(a, 'fsdp', [(i, i ^ r) for i in range(n)])]
    all_gather x4 -> x0, waiting for transfers between devices: 316 us -> none  [gather(): return lax.all_gather(w.astype(bf), 'fsdp', axis=0, tiled=True)]
    all_to_all x1 -> x0, blocking collectives: 218 us -> none  [scatter_sum(): q = lax.all_to_all(p, 'fsdp', 0, 0, tiled=True)]
    all_to_all x1 -> x0, waiting for transfers between devices: 201 us -> none  [scatter_sum(): q = lax.all_to_all(p, 'fsdp', 0, 0, tiled=True)]
    sub x2 -> x0, other arithmetic: 62.1 us -> none  [adam(): return (w - lr * (upd + wd * w), mn, vn)]
    convert_element_type x3 -> x0, other arithmetic: 51.9 us -> none  [gather(): return lax.all_gather(w.astype(bf), 'fsdp', axis=0, tiled=True)]
  transfers between devices with their start and end apart: 5 -> 48, of which waited for: 5 -> 13; matrix products, arithmetic and copies ran while one was open for 11% -> 20% of each run, Pallas kernels for 0% -> 40%
where the time goes in v1:
time: 1140 us
  Pallas kernels  510 us (45%)
  waiting for transfers between devices  356 us (31%)
  matrix products  206 us (18%)
  starting transfers between devices  35 us (3%)
  local copies, waits for them, and re-layouts  23.3 us (2%)
    ppermute x48, waiting for transfers between devices, hop(): return lax.ppermute(a, 'fsdp', [(i, i ^ r) for i in range(n)])  356 us
    pallas_call x4, Pallas kernels, hid(): pl.pallas_call(functools.partial(hid_kernel, n), grid_spec=pltpu.Prefetch...  199 us
    pallas_call x4, Pallas kernels, down(): pl.pallas_call(functools.partial(down_kernel, n), grid=(t // TM,), in_spe...  115 us
    pallas_call x4, Pallas kernels, up(): pl.pallas_call(functools.partial(up_kernel, n), grid_spec=pltpu.PrefetchS...  114 us
    dot_general x4, matrix products, back(): p1 = jnp.einsum('nd,nf->df', xl, dh, preferred_element_type=f32).astype(bf)  105 us
    dot_general x4, matrix products, back(): p2 = jnp.einsum('nf,nd->fd', a, gy, preferred_element_type=f32).astype(bf)  101 us
    pallas_call x4, Pallas kernels, adam(): pl.pallas_call(functools.partial(adam_kernel, n), grid_spec=pltpu.Prefetc...  65.4 us
    ppermute x48, starting transfers between devices, hop(): return lax.ppermute(a, 'fsdp', [(i, i ^ r) for i in range(n)])  35 us
  transfers between devices with their start and end apart: 48, of which 13 were waited for; matrix products, arithmetic and copies ran while one was open for 20% of the time, Pallas kernels for 40%

profile of v1, /device:TPU:0, one launch (start us, length us, event | category | flops | bytes accessed | tf_op | source)
XLA Modules:
  0.0 1135.6 jit_solution(6837277819966584214)
XLA Ops:
  19.0 41.7 %collective-permute-done.7.refs_2_.refs_6_ = bf16[768,1536]{1,0:T(8,128)(2,1)} collective-permute-done((bf16[768,1536]{1,0:T(8,128)(2,1)}, bf16[768,1536]{1,0:T(8,128)(2,1)}, u32[]{:S(2)}, u32[]{:S(2)}) %collective-permute-start.7) | collective-permute-done | bytes 2359328 | tf_op jit(solution)/shard_map/ppermute | solution.py:239
  69.6 41.6 %collective-permute-done.4.refs_2_.refs_6_ = bf16[768,1536]{1,0:T(8,128)(2,1)} collective-permute-done((bf16[768,1536]{1,0:T(8,128)(2,1)}, bf16[768,1536]{1,0:T(8,128)(2,1)}, u32[]{:S(2)}, u32[]{:S(2)}) %collective-permute-start.4) | collective-permute-done | bytes 2359328 | tf_op jit(solution)/shard_map/ppermute | solution.py:239
  113.3 48.5 %collective-permute-done.22.refs_2_.refs_6_ = bf16[768,1536]{1,0:T(8,128)(2,1)} collective-permute-done((bf16[768,1536]{1,0:T(8,128)(2,1)}, bf16[768,1536]{1,0:T(8,128)(2,1)}, u32[]{:S(2)}, u32[]{:S(2)}) %collective-permute-start.22) | collective-permute-done | bytes 2359328 | tf_op jit(solution)/shard_map/ppermute | solution.py:239
  162.3 49.6 %hid.4 = (bf16[4096,1536]{1,0:T(8,128)(2,1)}, bf16[4096,1536]{1,0:T(8,128)(2,1)}) custom-call(s32[1]{0:T(128)} %bitcast.me, bf16[4096,1536]{1,0:T(8,128)(2,1)} %bitcast.121, bf16[4096,1536]{1,0:T(8,128)(2,1)} %bitcast.125, bf16[768,1536]{1,0:T(8,128)(2,1)} %cast_chunk.6.refs_0_.refs_4_, bf16[768,1536]{1,0:T(8,128)(2,1)} %collective-permute-done.6.refs_1_.refs_5_, ...), custom_call_target="tpu_custom_call" | custom-call | flops 38654705664 | bytes 50331648 | tf_op jit(solution)/shard_map/hid/pallas_call | solution.py:98
  211.9 26.6 %convolution_convert_fusion.7 = bf16[1536,1536]{0,1:T(8,128)(2,1)S(1)} fusion(bf16[4096,1536]{1,0:T(8,128)(2,1)} %get-tuple-element.43, bf16[1,1,4096,1536]{3,2,1,0:T(8,128)(2,1)} %param.13), kind=kOutput, calls=%fused_computation.7 | convolution fusion | flops 19329712128 | bytes 29884416 | tf_op jit(solution)/shard_map/nd,nf->df/dot_general | solution.py:268
  240.6 24.0 %convolution_convert_fusion.6.refs_4_ = bf16[1536,1536]{1,0:T(8,128)(2,1)S(1)} fusion(bf16[4096,1536]{1,0:T(8,128)(2,1)S(1)} %copy-done.32, bf16[1,4096,1536]{2,1,0:T(8,128)(2,1)} %param.14), kind=kOutput, calls=%fused_computation.6 | convolution fusion | flops 19329712128 | bytes 29884416 | tf_op jit(solution)/shard_map/nf,nd->fd/dot_general | solution.py:267
  270.7 49.7 %hid.5 = (bf16[4096,1536]{1,0:T(8,128)(2,1)}, bf16[4096,1536]{1,0:T(8,128)(2,1)}) custom-call(s32[1]{0:T(128)} %bitcast.me, bf16[4096,1536]{1,0:T(8,128)(2,1)} %bitcast.122, bf16[4096,1536]{1,0:T(8,128)(2,1)} %bitcast.126, bf16[768,1536]{1,0:T(8,128)(2,1)} %cast_chunk.5.refs_0_.refs_4_, bf16[768,1536]{1,0:T(8,128)(2,1)} %collective-permute-done.3.refs_1_.refs_5_, ...), custom_call_target="tpu_custom_call" | custom-call | flops 38654705664 | bytes 50331648 | tf_op jit(solution)/shard_map/hid/pallas_call | solution.py:98
  320.5 26.2 %convolution_convert_fusion.5 = bf16[1536,1536]{0,1:T(8,128)(2,1)S(1)} fusion(bf16[4096,1536]{1,0:T(8,128)(2,1)} %get-tuple-element.45, bf16[1,1,4096,1536]{3,2,1,0:T(8,128)(2,1)} %param.13), kind=kOutput, calls=%fused_computation.5 | convolution fusion | flops 19329712128 | bytes 29884416 | tf_op jit(solution)/shard_map/nd,nf->df/dot_general | solution.py:268
  348.6 24.0 %convolution_convert_fusion.4.refs_4_ = bf16[1536,1536]{1,0:T(8,128)(2,1)S(1)} fusion(bf16[4096,1536]{1,0:T(8,128)(2,1)S(1)} %copy-done.33, bf16[1,4096,1536]{2,1,0:T(8,128)(2,1)} %param.14), kind=kOutput, calls=%fused_computation.4 | convolution fusion | flops 19329712128 | bytes 29884416 | tf_op jit(solution)/shard_map/nf,nd->fd/dot_general | solution.py:267
  376.9 49.8 %hid.6 = (bf16[4096,1536]{1,0:T(8,128)(2,1)}, bf16[4096,1536]{1,0:T(8,128)(2,1)}) custom-call(s32[1]{0:T(128)} %bitcast.me, bf16[4096,1536]{1,0:T(8,128)(2,1)} %bitcast.123, bf16[4096,1536]{1,0:T(8,128)(2,1)} %bitcast.127, bf16[768,1536]{1,0:T(8,128)(2,1)} %cast_chunk.7.refs_0_.refs_4_, bf16[768,1536]{1,0:T(8,128)(2,1)} %collective-permute-done.21.refs_1_.refs_5_, ...), custom_call_target="tpu_custom_call" | custom-call | flops 38654705664 | bytes 50331648 | tf_op jit(solution)/shard_map/hid/pallas_call | solution.py:98
  430.9 26.3 %convolution_convert_fusion.3 = bf16[1536,1536]{0,1:T(8,128)(2,1)S(1)} fusion(bf16[4096,1536]{1,0:T(8,128)(2,1)} %get-tuple-element.47, bf16[1,1,4096,1536]{3,2,1,0:T(8,128)(2,1)} %param.13), kind=kOutput, calls=%fused_computation.3 | convolution fusion | flops 19329712128 | bytes 29884416 | tf_op jit(solution)/shard_map/nd,nf->df/dot_general | solution.py:268
  457.3 23.0 %collective-permute-done.20.refs_7_ = bf16[384,1536]{1,0:T(8,128)(2,1)S(1)} collective-permute-done((bf16[384,1536]{1,0:T(8,128)(2,1)S(1)}, bf16[384,1536]{1,0:T(8,128)(2,1)S(1)}, u32[]{:S(2)}, u32[]{:S(2)}) %collective-permute-start.20) | collective-permute-done | bytes 1179680 | tf_op jit(solution)/shard_map/ppermute | solution.py:239
  480.7 25.5 %collective-permute-done.10.refs_2_ = bf16[384,1536]{1,0:T(8,128)(2,1)S(1)} collective-permute-done((bf16[384,1536]{1,0:T(8,128)(2,1)}, bf16[384,1536]{1,0:T(8,128)(2,1)S(1)}, u32[]{:S(2)}, u32[]{:S(2)}) %collective-permute-start.10) | collective-permute-done | bytes 1179680 | tf_op jit(solution)/shard_map/ppermute | solution.py:239
  508.1 22.9 %collective-permute-done.11.refs_3_ = bf16[384,1536]{1,0:T(8,128)(2,1)S(1)} collective-permute-done((bf16[384,1536]{1,0:T(8,128)(2,1)}, bf16[384,1536]{1,0:T(8,128)(2,1)S(1)}, u32[]{:S(2)}, u32[]{:S(2)}) %collective-permute-start.11) | collective-permute-done | bytes 1179680 | tf_op jit(solution)/shard_map/ppermute | solution.py:239
  532.8 26.6 %convolution_convert_fusion.2.refs_4_ = bf16[1536,1536]{1,0:T(8,128)(2,1)S(1)} fusion(bf16[4096,1536]{1,0:T(8,128)(2,1)} %get-tuple-element.48, bf16[1,4096,1536]{2,1,0:T(8,128)(2,1)} %param.14), kind=kOutput, calls=%fused_computation.2 | convolution fusion | flops 19329712128 | bytes 29884416 | tf_op jit(solution)/shard_map/nf,nd->fd/dot_general | solution.py:267
  582.7 16.5 %adam.5 = (f32[384,6144]{1,0:T(8,128)}, f32[384,6144]{1,0:T(8,128)}, f32[384,6144]{1,0:T(8,128)}, f32[1536,1536]{1,0:T(8,128)}, f32[1536,1536]{1,0:T(8,128)}, /*...) custom-call(s32[1]{0:T(128)} %bitcast.me, ...), custom_call_target="tpu_custom_call", output_to_operand_aliasing={{0}: (18, {}), {1}: (19, {}), {2}: (20, {}), {3}: (21, {}),... | custom-call | flops 35389440 | bytes 44826624 | tf_op jit(solution)/shard_map/adam/pallas_call | solution.py:219
  601.0 49.8 %hid.7 = (bf16[4096,1536]{1,0:T(8,128)(2,1)}, bf16[4096,1536]{1,0:T(8,128)(2,1)}) custom-call(s32[1]{0:T(128)} %bitcast.me, bf16[4096,1536]{1,0:T(8,128)(2,1)} %bitcast.124, bf16[4096,1536]{1,0:T(8,128)(2,1)} %bitcast.128, bf16[768,1536]{1,0:T(8,128)(2,1)} %cast_chunk.4.refs_0_.refs_4_, bf16[768,1536]{1,0:T(8,128)(2,1)} %collective-permute-done.refs_1_.refs_5_, ...), custom_call_target="tpu_custom_call" | custom-call | flops 38654705664 | bytes 50331648 | tf_op jit(solution)/shard_map/hid/pallas_call | solution.py:98
  650.8 26.2 %convolution_convert_fusion.1 = bf16[1536,1536]{0,1:T(8,128)(2,1)S(1)} fusion(bf16[4096,1536]{1,0:T(8,128)(2,1)} %get-tuple-element.57, bf16[1,1,4096,1536]{3,2,1,0:T(8,128)(2,1)} %param.13), kind=kOutput, calls=%fused_computation.1 | convolution fusion | flops 19329712128 | bytes 29884416 | tf_op jit(solution)/shard_map/nd,nf->df/dot_general | solution.py:268
  685.7 26.3 %convolution_convert_fusion.refs_4_ = bf16[1536,1536]{1,0:T(8,128)(2,1)S(1)} fusion(bf16[4096,1536]{1,0:T(8,128)(2,1)} %get-tuple-element.58, bf16[1,4096,1536]{2,1,0:T(8,128)(2,1)} %param.14), kind=kOutput, calls=%fused_computation | convolution fusion | flops 19329712128 | bytes 29884416 | tf_op jit(solution)/shard_map/nf,nd->fd/dot_general | solution.py:267
  716.9 18.3 %collective-permute-done.35.refs_7_ = bf16[384,1536]{1,0:T(8,128)(2,1)S(1)} collective-permute-done((bf16[384,1536]{1,0:T(8,128)(2,1)S(1)}, bf16[384,1536]{1,0:T(8,128)(2,1)S(1)}, u32[]{:S(2)}, u32[]{:S(2)}) %collective-permute-start.35) | collective-permute-done | bytes 1179680 | tf_op jit(solution)/shard_map/ppermute | solution.py:239
  754.2 32.6 %collective-permute-done.37.refs_2_ = bf16[768,1536]{1,0:T(8,128)(2,1)} collective-permute-done((bf16[768,1536]{1,0:T(8,128)(2,1)}, bf16[768,1536]{1,0:T(8,128)(2,1)}, u32[]{:S(2)}, u32[]{:S(2)}) %collective-permute-start.37) | collective-permute-done | bytes 2359328 | tf_op jit(solution)/shard_map/ppermute | solution.py:239
  788.7 28.3 %up.5.a = bf16[4096,1536]{1,0:T(8,128)(2,1)} custom-call(s32[1]{0:T(128)} %bitcast.me, bf16[4096,1536]{1,0:T(8,128)(2,1)} %bitcast.129, bf16[768,1536]{1,0:T(8,128)(2,1)} %get-tuple-element.55.refs_22_.refs_0_, bf16[768,1536]{1,0:T(8,128)(2,1)} %collective-permute-done.39.refs_1_, bf16[768,1536]{1,0:T(8,128)(2,1)} %collective-permute-done.40.refs_2_, ...), custom_call_target="tpu_custom_call" | custom-call | flops 19327352832 | bytes 25165824 | tf_op jit(solution)/shard_map/up/pallas_call | solution.py:130
  817.1 28.0 %down.4.acc = f32[4096,1536]{1,0:T(8,128)} custom-call(bf16[4096,1536]{1,0:T(8,128)(2,1)} %up.5.a, bf16[4096,1536]{1,0:T(8,128)(2,1)} %bitcast.130, bf16[768,1536]{1,0:T(8,128)(2,1)} %get-tuple-element.55.refs_22_.refs_0_, bf16[768,1536]{1,0:T(8,128)(2,1)} %collective-permute-done.39.refs_1_, bf16[768,1536]{1,0:T(8,128)(2,1)} %collective-permute-done.40.refs_2_, ...), custom_call_target="tpu_custom_call" | custom-call | flops 19327352832 | bytes 62914560 | tf_op jit(solution)/shard_map/down/pallas_call | solution.py:163
  846.7 28.3 %up.4.a = bf16[4096,1536]{1,0:T(8,128)(2,1)} custom-call(s32[1]{0:T(128)} %bitcast.me, bf16[4096,1536]{1,0:T(8,128)(2,1)} %bitcast.131, bf16[768,1536]{1,0:T(8,128)(2,1)} %get-tuple-element.56.refs_8_.refs_0_, bf16[768,1536]{1,0:T(8,128)(2,1)} %collective-permute-done.36.refs_1_, bf16[768,1536]{1,0:T(8,128)(2,1)} %collective-permute-done.37.refs_2_, ...), custom_call_target="tpu_custom_call" | custom-call | flops 19327352832 | bytes 25165824 | tf_op jit(solution)/shard_map/up/pallas_call | solution.py:130
  876.7 29.9 %down.5.refs_22_.acc = f32[4096,1536]{1,0:T(8,128)} custom-call(bf16[4096,1536]{1,0:T(8,128)(2,1)} %up.4.a, f32[4096,1536]{1,0:T(8,128)} %down.4.acc, bf16[768,1536]{1,0:T(8,128)(2,1)} %get-tuple-element.56.refs_8_.refs_0_, bf16[768,1536]{1,0:T(8,128)(2,1)} %collective-permute-done.36.refs_1_, bf16[768,1536]{1,0:T(8,128)(2,1)} %collective-permute-done.37.refs_2_, ...), custom_call_target="tpu_custom_call" | custom-call | flops 19327352832 | bytes 62914560 | tf_op jit(solution)/shard_map/down/pallas_call | solution.py:163
  906.6 19.4 %collective-permute-done.28.refs_6_ = bf16[384,1536]{1,0:T(8,128)(2,1)} collective-permute-done((bf16[384,1536]{1,0:T(8,128)(2,1)S(1)}, bf16[384,1536]{1,0:T(8,128)(2,1)}, u32[]{:S(2)}, u32[]{:S(2)}) %collective-permute-start.28) | collective-permute-done | bytes 1179680 | tf_op jit(solution)/shard_map/ppermute | solution.py:239
  926.0 23.4 %collective-permute-done.29.refs_7_ = bf16[384,1536]{1,0:T(8,128)(2,1)} collective-permute-done((bf16[384,1536]{1,0:T(8,128)(2,1)S(1)}, bf16[384,1536]{1,0:T(8,128)(2,1)}, u32[]{:S(2)}, u32[]{:S(2)}) %collective-permute-start.29) | collective-permute-done | bytes 1179680 | tf_op jit(solution)/shard_map/ppermute | solution.py:239
  967.3 52.8 %collective-permute-done.43.refs_2_ = bf16[768,1536]{1,0:T(8,128)(2,1)} collective-permute-done((bf16[768,1536]{1,0:T(8,128)(2,1)}, bf16[768,1536]{1,0:T(8,128)(2,1)}, u32[]{:S(2)}, u32[]{:S(2)}) %collective-permute-start.43) | collective-permute-done | bytes 2359328 | tf_op jit(solution)/shard_map/ppermute | solution.py:239
  1021.5 28.3 %up.6.a = bf16[4096,1536]{1,0:T(8,128)(2,1)} custom-call(s32[1]{0:T(128)} %bitcast.me, bf16[4096,1536]{1,0:T(8,128)(2,1)} %bitcast.132, bf16[768,1536]{1,0:T(8,128)(2,1)} %get-tuple-element.71.refs_4_.refs_0_, bf16[768,1536]{1,0:T(8,128)(2,1)} %copy-done.17, bf16[768,1536]{1,0:T(8,128)(2,1)} %collective-permute-done.46.refs_2_, ...), custom_call_target="tpu_custom_call" | custom-call | flops 19327352832 | bytes 25165824 | tf_op jit(solution)/shard_map/up/pallas_call | solution.py:130
  1049.8 29.8 %down.6.refs_4_.acc = f32[4096,1536]{1,0:T(8,128)} custom-call(bf16[4096,1536]{1,0:T(8,128)(2,1)} %up.6.a, f32[4096,1536]{1,0:T(8,128)} %down.5.refs_22_.acc, bf16[768,1536]{1,0:T(8,128)(2,1)} %get-tuple-element.71.refs_4_.refs_0_, bf16[768,1536]{1,0:T(8,128)(2,1)} %copy-done.17, bf16[768,1536]{1,0:T(8,128)(2,1)} %collective-permute-done.46.refs_2_, ...), custom_call_target="tpu_custom_call" | custom-call | flops 19327352832 | bytes 62914560 | tf_op jit(solution)/shard_map/down/pallas_call | solution.py:163
  1079.6 28.6 %up.7.a = bf16[4096,1536]{1,0:T(8,128)(2,1)} custom-call(s32[1]{0:T(128)} %bitcast.me, bf16[4096,1536]{1,0:T(8,128)(2,1)} %bitcast.133, bf16[768,1536]{1,0:T(8,128)(2,1)} %get-tuple-element.78.refs_4_.refs_0_, bf16[768,1536]{1,0:T(8,128)(2,1)} %collective-permute-done.42.refs_1_, bf16[768,1536]{1,0:T(8,128)(2,1)} %collective-permute-done.43.refs_2_, ...), custom_call_target="tpu_custom_call" | custom-call | flops 19327352832 | bytes 25165824 | tf_op jit(solution)/shard_map/up/pallas_call | solution.py:130
  1108.2 27.2 %down.7 = bf16[4096,1536]{1,0:T(8,128)(2,1)} custom-call(bf16[4096,1536]{1,0:T(8,128)(2,1)} %up.7.a, f32[4096,1536]{1,0:T(8,128)} %down.6.refs_4_.acc, bf16[768,1536]{1,0:T(8,128)(2,1)} %get-tuple-element.78.refs_4_.refs_0_, bf16[768,1536]{1,0:T(8,128)(2,1)} %collective-permute-done.42.refs_1_, bf16[768,1536]{1,0:T(8,128)(2,1)} %collective-permute-done.43.refs_2_, ...), custom_call_target="tpu_custom_call" | custom-call | flops 19327352832 | bytes 62914560 | tf_op jit(solution)/shard_map/down/pallas_call | solution.py:163
  (170 shorter events, 132.5 us)
Async XLA Ops:
  12.6 98.6 %collective-permute-start.4 = (bf16[768,1536]{1,0:T(8,128)(2,1)}, bf16[768,1536]{1,0:T(8,128)(2,1)}, u32[]{:S(2)}, u32[]{:S(2)}) collective-permute-start(bf16[768,1536]{1,0:T(8,128)(2,1)} %cast_chunk.5.refs_0_.refs_4_), channel_id=1, source_target_pairs={{0,2},{1,3},{2,0},{3,1},{4,6},{5,7},{6,4},{7,5}} | collective-permute-start | bytes 7077896 | tf_op jit(solution)/shard_map/ppermute | solution.py:239
  17.1 144.7 %collective-permute-start.22 = (bf16[768,1536]{1,0:T(8,128)(2,1)}, bf16[768,1536]{1,0:T(8,128)(2,1)}, u32[]{:S(2)}, u32[]{:S(2)}) collective-permute-start(bf16[768,1536]{1,0:T(8,128)(2,1)} %cast_chunk.7.refs_0_.refs_4_), channel_id=1, source_target_pairs={{0,2},{1,3},{2,0},{3,1},{4,6},{5,7},{6,4},{7,5}} | collective-permute-start | bytes 7077896 | tf_op jit(solution)/shard_map/ppermute | solution.py:239
  60.7 101.1 %collective-permute-start.8 = (bf16[768,1536]{1,0:T(8,128)(2,1)}, bf16[768,1536]{1,0:T(8,128)(2,1)}, u32[]{:S(2)}, u32[]{:S(2)}) collective-permute-start(bf16[768,1536]{1,0:T(8,128)(2,1)} %collective-permute-done.7.refs_2_.refs_6_), channel_id=1, source_target_pairs={{0,1},{1,0},{2,3},{3,2},{4,5},{5,4},{6,7},{7,6}} | collective-permute-start | bytes 7077896 | tf_op jit(solution)/shard_map/ppermute | solution.py:239
  60.7 208.0 %collective-permute-start.3 = (bf16[768,1536]{1,0:T(8,128)(2,1)S(1)}, bf16[768,1536]{1,0:T(8,128)(2,1)}, u32[]{:S(2)}, u32[]{:S(2)}) collective-permute-start(bf16[768,1536]{1,0:T(8,128)(2,1)S(1)} %copy-done.18), channel_id=1, source_target_pairs={{0,1},{1,0},{2,3},{3,2},{4,5},{5,4},{6,7},{7,6}} | collective-permute-start | bytes 7077896 | tf_op jit(solution)/shard_map/ppermute | solution.py:239
  69.6 307.1 %collective-permute-start.21 = (bf16[768,1536]{1,0:T(8,128)(2,1)}, bf16[768,1536]{1,0:T(8,128)(2,1)}, u32[]{:S(2)}, u32[]{:S(2)}) collective-permute-start(bf16[768,1536]{1,0:T(8,128)(2,1)} %cast_chunk.7.refs_0_.refs_4_), channel_id=1, source_target_pairs={{0,1},{1,0},{2,3},{3,2},{4,5},{5,4},{6,7},{7,6}} | collective-permute-start | bytes 7077896 | tf_op jit(solution)/shard_map/ppermute | solution.py:239
  111.2 315.5 %collective-permute-start.1 = (bf16[768,1536]{1,0:T(8,128)(2,1)}, bf16[768,1536]{1,0:T(8,128)(2,1)}, u32[]{:S(2)}, u32[]{:S(2)}) collective-permute-start(bf16[768,1536]{1,0:T(8,128)(2,1)} %cast_chunk.4.refs_0_.refs_4_), channel_id=1, source_target_pairs={{0,2},{1,3},{2,0},{3,1},{4,6},{5,7},{6,4},{7,5}} | collective-permute-start | bytes 7077896 | tf_op jit(solution)/shard_map/ppermute | solution.py:239
  161.8 106.9 %collective-permute-start.5 = (bf16[768,1536]{1,0:T(8,128)(2,1)}, bf16[768,1536]{1,0:T(8,128)(2,1)}, u32[]{:S(2)}, u32[]{:S(2)}) collective-permute-start(bf16[768,1536]{1,0:T(8,128)(2,1)} %collective-permute-done.4.refs_2_.refs_6_), channel_id=1, source_target_pairs={{0,1},{1,0},{2,3},{3,2},{4,5},{5,4},{6,7},{7,6}} | collective-permute-start | bytes 7077896 | tf_op jit(solution)/shard_map/ppermute | solution.py:239
  161.8 215.0 %collective-permute-start.23 = (bf16[768,1536]{1,0:T(8,128)(2,1)}, bf16[768,1536]{1,0:T(8,128)(2,1)}, u32[]{:S(2)}, u32[]{:S(2)}) collective-permute-start(bf16[768,1536]{1,0:T(8,128)(2,1)} %collective-permute-done.22.refs_2_.refs_6_), channel_id=1, source_target_pairs={{0,1},{1,0},{2,3},{3,2},{4,5},{5,4},{6,7},{7,6}} | collective-permute-start | bytes 7077896 | tf_op jit(solution)/shard_map/ppermute | solution.py:239
  268.7 160.0 %collective-permute-start.15 = (bf16[384,1536]{1,0:T(8,128)(2,1)}, bf16[384,1536]{1,0:T(8,128)(2,1)}, u32[]{:S(2)}, u32[]{:S(2)}) collective-permute-start(bf16[384,1536]{1,0:T(8,128)(2,1)} %get-tuple-element.102.refs_8_), channel_id=1, source_target_pairs={{0,1},{1,0},{2,3},{3,2},{4,5},{5,4},{6,7},{7,6}} | collective-permute-start | bytes 3538952 | tf_op jit(solution)/shard_map/ppermute | solution.py:239
  268.7 160.0 %collective-permute-start.16 = (bf16[384,1536]{1,0:T(8,128)(2,1)}, bf16[384,1536]{1,0:T(8,128)(2,1)}, u32[]{:S(2)}, u32[]{:S(2)}) collective-permute-start(bf16[384,1536]{1,0:T(8,128)(2,1)} %get-tuple-element.101.refs_9_), channel_id=1, source_target_pairs={{0,2},{1,3},{2,0},{3,1},{4,6},{5,7},{6,4},{7,5}} | collective-permute-start | bytes 3538952 | tf_op jit(solution)/shard_map/ppermute | solution.py:239
  428.7 77.5 %collective-permute-start.10 = (bf16[384,1536]{1,0:T(8,128)(2,1)}, bf16[384,1536]{1,0:T(8,128)(2,1)S(1)}, u32[]{:S(2)}, u32[]{:S(2)}) collective-permute-start(bf16[384,1536]{1,0:T(8,128)(2,1)} %get-tuple-element.95.refs_9_), channel_id=1, source_target_pairs={{0,2},{1,3},{2,0},{3,1},{4,6},{5,7},{6,4},{7,5}} | collective-permute-start | bytes 3538952 | tf_op jit(solution)/shard_map/ppermute | solution.py:239
  430.2 100.7 %collective-permute-start.11 = (bf16[384,1536]{1,0:T(8,128)(2,1)}, bf16[384,1536]{1,0:T(8,128)(2,1)S(1)}, u32[]{:S(2)}, u32[]{:S(2)}) collective-permute-start(bf16[384,1536]{1,0:T(8,128)(2,1)} %get-tuple-element.94.refs_10_), channel_id=1, source_target_pairs={{0,3},{1,2},{2,1},{3,0},{4,7},{5,6},{6,5},{7,4}} | collective-permute-start | bytes 3538952 | tf_op jit(solution)/shard_map/ppermute | solution.py:239
  430.5 102.3 %collective-permute-start.12 = (bf16[384,1536]{1,0:T(8,128)(2,1)}, bf16[384,1536]{1,0:T(8,128)(2,1)S(1)}, u32[]{:S(2)}, u32[]{:S(2)}) collective-permute-start(bf16[384,1536]{1,0:T(8,128)(2,1)} %get-tuple-element.93.refs_11_), channel_id=1, source_target_pairs={{0,1},{1,0},{2,3},{3,2},{4,5},{5,4},{6,7},{7,6}} | collective-permute-start | bytes 3538952 | tf_op jit(solution)/shard_map/ppermute | solution.py:239
  457.2 142.0 %collective-permute-start = (bf16[768,1536]{1,0:T(8,128)(2,1)}, bf16[768,1536]{1,0:T(8,128)(2,1)}, u32[]{:S(2)}, u32[]{:S(2)}) collective-permute-start(bf16[768,1536]{1,0:T(8,128)(2,1)} %cast_chunk.4.refs_0_.refs_4_), channel_id=1, source_target_pairs={{0,1},{1,0},{2,3},{3,2},{4,5},{5,4},{6,7},{7,6}} | collective-permute-start | bytes 7077896 | tf_op jit(solution)/shard_map/ppermute | solution.py:239
  480.3 119.2 %collective-permute-start.2 = (bf16[768,1536]{1,0:T(8,128)(2,1)}, bf16[768,1536]{1,0:T(8,128)(2,1)}, u32[]{:S(2)}, u32[]{:S(2)}) collective-permute-start(bf16[768,1536]{1,0:T(8,128)(2,1)} %collective-permute-done.1.refs_2_.refs_6_), channel_id=1, source_target_pairs={{0,1},{1,0},{2,3},{3,2},{4,5},{5,4},{6,7},{7,6}} | collective-permute-start | bytes 7077896 | tf_op jit(solution)/shard_map/ppermute | solution.py:239
  506.2 73.9 %collective-permute-start.13 = (bf16[384,1536]{1,0:T(8,128)(2,1)}, bf16[384,1536]{1,0:T(8,128)(2,1)}, u32[]{:S(2)}, u32[]{:S(2)}) collective-permute-start(bf16[384,1536]{1,0:T(8,128)(2,1)} %get-tuple-element.92.refs_12_), channel_id=1, source_target_pairs={{0,2},{1,3},{2,0},{3,1},{4,6},{5,7},{6,4},{7,5}} | collective-permute-start | bytes 3538952 | tf_op jit(solution)/shard_map/ppermute | solution.py:239
  580.1 96.9 %collective-permute-start.30 = (bf16[384,1536]{1,0:T(8,128)(2,1)}, bf16[384,1536]{1,0:T(8,128)(2,1)}, u32[]{:S(2)}, u32[]{:S(2)}) collective-permute-start(bf16[384,1536]{1,0:T(8,128)(2,1)} %get-tuple-element.90.refs_16_), channel_id=1, source_target_pairs={{0,1},{1,0},{2,3},{3,2},{4,5},{5,4},{6,7},{7,6}} | collective-permute-start | bytes 3538952 | tf_op jit(solution)/shard_map/ppermute | solution.py:239
  580.9 96.7 %collective-permute-start.31 = (bf16[384,1536]{1,0:T(8,128)(2,1)S(1)}, bf16[384,1536]{1,0:T(8,128)(2,1)}, u32[]{:S(2)}, u32[]{:S(2)}) collective-permute-start(bf16[384,1536]{1,0:T(8,128)(2,1)S(1)} %copy-done.12), channel_id=1, source_target_pairs={{0,2},{1,3},{2,0},{3,1},{4,6},{5,7},{6,4},{7,5}} | collective-permute-start | bytes 3538952 | tf_op jit(solution)/shard_map/ppermute | solution.py:239
  582.5 96.1 %collective-permute-start.32 = (bf16[384,1536]{1,0:T(8,128)(2,1)S(1)}, bf16[384,1536]{1,0:T(8,128)(2,1)}, u32[]{:S(2)}, u32[]{:S(2)}) collective-permute-start(bf16[384,1536]{1,0:T(8,128)(2,1)S(1)} %copy-done.11), channel_id=1, source_target_pairs={{0,3},{1,2},{2,1},{3,0},{4,7},{5,6},{6,5},{7,4}} | collective-permute-start | bytes 3538952 | tf_op jit(solution)/shard_map/ppermute | solution.py:239
  599.2 80.0 %collective-permute-start.33 = (bf16[384,1536]{1,0:T(8,128)(2,1)S(1)}, bf16[384,1536]{1,0:T(8,128)(2,1)}, u32[]{:S(2)}, u32[]{:S(2)}) collective-permute-start(bf16[384,1536]{1,0:T(8,128)(2,1)S(1)} %copy-done.10), channel_id=1, source_target_pairs={{0,1},{1,0},{2,3},{3,2},{4,5},{5,4},{6,7},{7,6}} | collective-permute-start | bytes 3538952 | tf_op jit(solution)/shard_map/ppermute | solution.py:239
  599.5 86.2 %collective-permute-start.40 = (bf16[768,1536]{1,0:T(8,128)(2,1)}, bf16[768,1536]{1,0:T(8,128)(2,1)}, u32[]{:S(2)}, u32[]{:S(2)}) collective-permute-start(bf16[768,1536]{1,0:T(8,128)(2,1)} %get-tuple-element.55.refs_22_.refs_0_), channel_id=1, source_target_pairs={{0,2},{1,3},{2,0},{3,1},{4,6},{5,7},{6,4},{7,5}} | collective-permute-start | bytes 7077896 | tf_op jit(solution)/shard_map/ppermute | solution.py:239
  678.5 74.0 %collective-permute-start.39 = (bf16[768,1536]{1,0:T(8,128)(2,1)}, bf16[768,1536]{1,0:T(8,128)(2,1)}, u32[]{:S(2)}, u32[]{:S(2)}) collective-permute-start(bf16[768,1536]{1,0:T(8,128)(2,1)} %get-tuple-element.55.refs_22_.refs_0_), channel_id=1, source_target_pairs={{0,1},{1,0},{2,3},{3,2},{4,5},{5,4},{6,7},{7,6}} | collective-permute-start | bytes 7077896 | tf_op jit(solution)/shard_map/ppermute | solution.py:239
  679.2 107.6 %collective-permute-start.37 = (bf16[768,1536]{1,0:T(8,128)(2,1)}, bf16[768,1536]{1,0:T(8,128)(2,1)}, u32[]{:S(2)}, u32[]{:S(2)}) collective-permute-start(bf16[768,1536]{1,0:T(8,128)(2,1)} %get-tuple-element.56.refs_8_.refs_0_), channel_id=1, source_target_pairs={{0,2},{1,3},{2,0},{3,1},{4,6},{5,7},{6,4},{7,5}} | collective-permute-start | bytes 7077896 | tf_op jit(solution)/shard_map/ppermute | solution.py:239
  685.7 101.6 %collective-permute-start.41 = (bf16[768,1536]{1,0:T(8,128)(2,1)}, bf16[768,1536]{1,0:T(8,128)(2,1)S(1)}, u32[]{:S(2)}, u32[]{:S(2)}) collective-permute-start(bf16[768,1536]{1,0:T(8,128)(2,1)} %collective-permute-done.40.refs_2_), channel_id=1, source_target_pairs={{0,1},{1,0},{2,3},{3,2},{4,5},{5,4},{6,7},{7,6}} | collective-permute-start | bytes 7077896 | tf_op jit(solution)/shard_map/ppermute | solution.py:239
  716.4 128.7 %collective-permute-start.36 = (bf16[768,1536]{1,0:T(8,128)(2,1)}, bf16[768,1536]{1,0:T(8,128)(2,1)}, u32[]{:S(2)}, u32[]{:S(2)}) collective-permute-start(bf16[768,1536]{1,0:T(8,128)(2,1)} %get-tuple-element.56.refs_8_.refs_0_), channel_id=1, source_target_pairs={{0,1},{1,0},{2,3},{3,2},{4,5},{5,4},{6,7},{7,6}} | collective-permute-start | bytes 7077896 | tf_op jit(solution)/shard_map/ppermute | solution.py:239
  735.2 139.9 %collective-permute-start.24 = (bf16[384,1536]{1,0:T(8,128)(2,1)}, bf16[384,1536]{1,0:T(8,128)(2,1)}, u32[]{:S(2)}, u32[]{:S(2)}) collective-permute-start(bf16[384,1536]{1,0:T(8,128)(2,1)} %get-tuple-element.84.refs_22_), channel_id=1, source_target_pairs={{0,1},{1,0},{2,3},{3,2},{4,5},{5,4},{6,7},{7,6}} | collective-permute-start | bytes 3538952 | tf_op jit(solution)/shard_map/ppermute | solution.py:239
  752.5 124.2 %collective-permute-start.25 = (bf16[384,1536]{1,0:T(8,128)(2,1)}, bf16[384,1536]{1,0:T(8,128)(2,1)}, u32[]{:S(2)}, u32[]{:S(2)}) collective-permute-start(bf16[384,1536]{1,0:T(8,128)(2,1)} %get-tuple-element.83.refs_23_), channel_id=1, source_target_pairs={{0,2},{1,3},{2,0},{3,1},{4,6},{5,7},{6,4},{7,5}} | collective-permute-start | bytes 3538952 | tf_op jit(solution)/shard_map/ppermute | solution.py:239
  786.8 119.8 %collective-permute-start.26 = (bf16[384,1536]{1,0:T(8,128)(2,1)}, bf16[384,1536]{1,0:T(8,128)(2,1)}, u32[]{:S(2)}, u32[]{:S(2)}) collective-permute-start(bf16[384,1536]{1,0:T(8,128)(2,1)} %get-tuple-element.82.refs_24_), channel_id=1, source_target_pairs={{0,3},{1,2},{2,1},{3,0},{4,7},{5,6},{6,5},{7,4}} | collective-permute-start | bytes 3538952 | tf_op jit(solution)/shard_map/ppermute | solution.py:239
  845.1 61.5 %collective-permute-start.27 = (bf16[384,1536]{1,0:T(8,128)(2,1)S(1)}, bf16[384,1536]{1,0:T(8,128)(2,1)}, u32[]{:S(2)}, u32[]{:S(2)}) collective-permute-start(bf16[384,1536]{1,0:T(8,128)(2,1)S(1)} %copy-done.15), channel_id=1, source_target_pairs={{0,1},{1,0},{2,3},{3,2},{4,5},{5,4},{6,7},{7,6}} | collective-permute-start | bytes 3538952 | tf_op jit(solution)/shard_map/ppermute | solution.py:239
  846.3 120.5 %collective-permute-start.46 = (bf16[768,1536]{1,0:T(8,128)(2,1)}, bf16[768,1536]{1,0:T(8,128)(2,1)}, u32[]{:S(2)}, u32[]{:S(2)}) collective-permute-start(bf16[768,1536]{1,0:T(8,128)(2,1)} %get-tuple-element.71.refs_4_.refs_0_), channel_id=1, source_target_pairs={{0,2},{1,3},{2,0},{3,1},{4,6},{5,7},{6,4},{7,5}} | collective-permute-start | bytes 7077896 | tf_op jit(solution)/shard_map/ppermute | solution.py:239
  876.7 72.7 %collective-permute-start.29 = (bf16[384,1536]{1,0:T(8,128)(2,1)S(1)}, bf16[384,1536]{1,0:T(8,128)(2,1)}, u32[]{:S(2)}, u32[]{:S(2)}) collective-permute-start(bf16[384,1536]{1,0:T(8,128)(2,1)S(1)} %copy-done.13), channel_id=1, source_target_pairs={{0,3},{1,2},{2,1},{3,0},{4,7},{5,6},{6,5},{7,4}} | collective-permute-start | bytes 3538952 | tf_op jit(solution)/shard_map/ppermute | solution.py:239
  966.8 112.8 %collective-permute-start.42 = (bf16[768,1536]{1,0:T(8,128)(2,1)}, bf16[768,1536]{1,0:T(8,128)(2,1)}, u32[]{:S(2)}, u32[]{:S(2)}) collective-permute-start(bf16[768,1536]{1,0:T(8,128)(2,1)} %get-tuple-element.78.refs_4_.refs_0_), channel_id=1, source_target_pairs={{0,1},{1,0},{2,3},{3,2},{4,5},{5,4},{6,7},{7,6}} | collective-permute-start | bytes 7077896 | tf_op jit(solution)/shard_map/ppermute | solution.py:239
  (50 other events, 1919.0 us)

commit v2 on v1

--- a/solution.py
+++ b/solution.py
@@ -51,13 +51,14 @@
         name="cast_chunk", compiler_params=params())(w1, w2)
 
 
-def join1(me, cs, n, w1):
+def join1(me, cs, n, w1, qs):
     b = cs[0].shape[0]
     w = w1.shape[1] // n
-    for q in range(n):
+    for q, c in zip(qs, cs):
+        i = pl.multiple_of(((me ^ q) % len(qs)) * b, 128)
         for r in range(n):
             j = pl.multiple_of((me ^ r) * w, 128)
-            w1[pl.ds(pl.multiple_of((me ^ q) * b, 128), b), r * w:(r + 1) * w] = cs[q][:, pl.ds(j, w)]
+            w1[pl.ds(i, b), r * w:(r + 1) * w] = c[:, pl.ds(j, w)]
 
 
 def join2(cs, n, w2):
@@ -72,7 +73,7 @@
 
     @pl.when(pl.program_id(0) == 0)
     def _():
-        join1(me[0], c1, n, w1)
+        join1(me[0], c1, n, w1, range(n))
         join2(c2, n, w2)
 
     xv = x[...]
@@ -107,42 +108,51 @@
         name="hid", compiler_params=params())(me, x, dy, *cs, *cs, *after)
 
 
-def up_kernel(n, me, x, *refs):
-    c1 = refs[:n]
+def up_kernel(n, qs, me, x, *refs):
+    c1 = refs[:len(qs)]
     a_out, w1 = refs[-2:]
+    part = refs[len(qs)] if qs[0] else None
 
     @pl.when(pl.program_id(0) == 0)
     def _():
-        join1(me[0], c1, n, w1)
+        join1(me[0], c1, n, w1, qs)
 
     xv = x[...]
     for s in range(0, w1.shape[1], TN):
         h = jnp.dot(xv, w1[:, s:s + TN], preferred_element_type=f32)
-        t = jnp.tanh(h * (C0 + (C0 * C1) * (h * h)))
-        a_out[:, s:s + TN] = (h * (0.5 + 0.5 * t)).astype(bf)
-
-
-def up(me, x, cs, after):
-    n = len(cs)
+        if part is not None:
+            h = part[:, s:s + TN] + h
+        if a_out.dtype == f32:
+            a_out[:, s:s + TN] = h
+        else:
+            t = jnp.tanh(h * (C0 + (C0 * C1) * (h * h)))
+            a_out[:, s:s + TN] = (h * (0.5 + 0.5 * t)).astype(bf)
+
+
+def up(me, x, cs, n, qs, part, after):
     t, d = x.shape
-    h2, w = cs[0].shape
-    hh = h2 // 2
+    hh = d // n
+    w = cs[0].shape[1]
+    half = len(qs) // 2 if len(qs) < n else 0
+    dk = d * len(qs) // n
+    side = pl.BlockSpec((TM, dk), lambda i, me: (i, ((me[0] ^ qs[0]) // len(qs))))
+    tok = pl.BlockSpec((TM, w), lambda i, *_: (i, 0))
+    extra = [] if part is None else [part]
     return pl.pallas_call(
-        functools.partial(up_kernel, n),
+        functools.partial(up_kernel, n, qs),
         grid_spec=pltpu.PrefetchScalarGridSpec(
             num_scalar_prefetch=1, grid=(t // TM,),
-            in_specs=[pl.BlockSpec((TM, d), lambda i, *_: (i, 0))] + [whole((hh, w))] * n
-            + [LATER] * len(after),
-            out_specs=pl.BlockSpec((TM, w), lambda i, *_: (i, 0)),
-            scratch_shapes=[pltpu.VMEM((n * hh, w), bf)]),
-        out_shape=jax.ShapeDtypeStruct((t, w), bf),
-        cost_estimate=cost(2 * t * d * w, 4 * t * d),
-        name="up", compiler_params=params())(me, x, *cs, *after)
+            in_specs=[side] + [whole((hh, w))] * len(qs) + [tok] * len(extra) + [LATER] * len(after),
+            out_specs=tok,
+            scratch_shapes=[pltpu.VMEM((dk, w), bf)]),
+        out_shape=jax.ShapeDtypeStruct((t, w), f32 if half and part is None else bf),
+        cost_estimate=cost(2 * t * dk * w, 4 * t * d),
+        name="up", compiler_params=params())(me, x, *cs, *extra, *after)
 
 
 def down_kernel(n, a, acc, *refs):
     c2 = refs[:n]
-    out, w2 = refs[n:]
+    out, w2 = refs[-2:]
 
     @pl.when(pl.program_id(0) == 0)
     def _():
@@ -154,30 +164,28 @@
         out[:, s:s + TN] = (acc[:, s:s + TN].astype(f32) + o).astype(out.dtype)
 
 
-def down(a, acc, cs, dtype):
+def down(a, acc, cs, row, side, dtype):
     n = len(cs)
-    t, w = a.shape
-    h2, d = cs[0].shape
-    hh = h2 // 2
+    t, d = acc.shape
+    hh = cs[0].shape[0] // (row + 1)
     tok = pl.BlockSpec((TM, d), lambda i: (i, 0))
     return pl.pallas_call(
         functools.partial(down_kernel, n), grid=(t // TM,),
-        in_specs=[pl.BlockSpec((TM, w), lambda i: (i, 0)), tok] + [whole((hh, d), 1)] * n,
+        in_specs=[pl.BlockSpec((TM, n * hh), lambda i: (i, side)), tok] + [whole((hh, d), row)] * n,
         out_specs=tok,
         scratch_shapes=[pltpu.VMEM((n * hh, d), bf)],
         out_shape=jax.ShapeDtypeStruct((t, d), dtype),
-        cost_estimate=cost(2 * t * d * w, 10 * t * d),
+        cost_estimate=cost(2 * t * d * n * hh, 10 * t * d),
         name="down", compiler_params=params())(a, acc, *cs)
 
 
-def adam_kernel(n, me, sc, *refs):
+def adam_kernel(n, halves, me, sc, *refs):
     lr, b1, b2, eps, wd, u1, u2 = (sc[i] for i in range(7))
-    p1, p2 = refs[:n], refs[n:2 * n]
-    wi = refs[2 * n:2 * n + 8]
-    outs = refs[-7:]
-    b = outs[6].shape[0] // 2
-    for half, ps in ((0, p1), (1, p2)):
-        w, ga, m, v = (wi[half * 4 + i][...] for i in range(4))
+    outs = refs[-3 * halves - 1:]
+    b = outs[-1].shape[0] // halves
+    for half in range(halves):
+        ps = refs[half * n:(half + 1) * n]
+        w, ga, m, v = (refs[halves * n + half * 4 + i][...] for i in range(4))
         s = ps[0][...].astype(f32)
         for q in range(1, n):
             s = s + ps[q][...].astype(f32)
@@ -189,44 +197,44 @@
         outs[half * 3][...] = wn
         outs[half * 3 + 1][...] = mn
         outs[half * 3 + 2][...] = vn
-        outs[6][half * b:(half + 1) * b, :] = wn.astype(bf)
-
-
-def adam(me, sc, p1, got1, p2, got2, st1, st2, prev, k, after):
-    n = len(got1) + 1
-    r, ff = st1[0].shape
-    f, d = st2[0].shape
-    cb, rb, dc = ff // (n * NK), f // NK, d // n
-
-    def col(q):
-        return pl.BlockSpec((r, cb), lambda j, me, sc: (0 if q else me[0], me[0] ^ q ^ j))
-
-    def straight():
-        return pl.BlockSpec((rb, dc), lambda j, me, sc: (0, j))
-
-    s1 = pl.BlockSpec((r, cb), lambda j, me, sc: (0, j * NK + k))
-    s2 = pl.BlockSpec((rb, dc), lambda j, me, sc: (k, j))
-    specs = ([col(q) for q in range(n)] + [straight()] * n
-             + [s1] * 4 + [s2] * 4)
-    args = [p1] + got1 + [p2] + got2 + st1 + st2
-    alias = {}
-    if prev is not None:
-        alias = {2 + len(args) + i: i for i in range(6)}
-        specs = specs + [pl.BlockSpec(memory_space=pl.ANY)] * 6
-        args = args + prev
-    specs = specs + [LATER] * len(after)
-    args = args + after
+        outs[-1][half * b:(half + 1) * b, :] = wn.astype(bf)
+
+
+def adam(me, sc, n, k, jobs, after):
+    specs, args, states, state_specs, outs, out_specs, done = [], [], [], [], [], [], []
+    rows = 0
+    for which, ps, st, prev in jobs:
+        r, c = st[0].shape
+        if which == 1:
+            rb, cb = r, c // (n * NK)
+            spec = pl.BlockSpec((rb, cb), lambda j, me, sc: (0, j * NK + k))
+            specs += [pl.BlockSpec((rb, cb), lambda j, me, sc, q=q: (0 if q else me[0], me[0] ^ q ^ j))
+                      for q in range(n)]
+        else:
+            rb, cb = r // NK, c // n
+            spec = pl.BlockSpec((rb, cb), lambda j, me, sc: (k, j))
+            specs += [pl.BlockSpec((rb, cb), lambda j, me, sc: (0, j))] * n
+        args += ps
+        states += st
+        state_specs += [spec] * 4
+        outs += [jax.ShapeDtypeStruct((r, c), f32)] * 3
+        out_specs += [spec] * 3
+        done += prev or []
+        rows += rb
+    args += states
+    alias = {2 + len(args) + i: i for i in range(len(done))}
+    args += done + after
+    specs += state_specs + [LATER] * (len(done) + len(after))
     out = pl.pallas_call(
-        functools.partial(adam_kernel, n),
+        functools.partial(adam_kernel, n, len(jobs)),
         grid_spec=pltpu.PrefetchScalarGridSpec(
             num_scalar_prefetch=2, grid=(n,), in_specs=specs,
-            out_specs=[s1] * 3 + [s2] * 3 + [pl.BlockSpec((r + rb, cb), lambda j, me, sc: (0, j))]),
-        out_shape=[jax.ShapeDtypeStruct((r, ff), f32)] * 3
-        + [jax.ShapeDtypeStruct((f, d), f32)] * 3 + [jax.ShapeDtypeStruct((r + rb, d), bf)],
+            out_specs=out_specs + [pl.BlockSpec((rows, cb), lambda j, me, sc: (0, j))]),
+        out_shape=outs + [jax.ShapeDtypeStruct((rows, n * cb), bf)],
         input_output_aliases=alias,
-        cost_estimate=cost(r * d * 60, r * d * 76),
+        cost_estimate=cost(rows * n * cb * 30, rows * n * cb * 38),
         name="adam", compiler_params=params())(me, sc, *args)
-    return list(out[:6]), out[6]
+    return [list(out[3 * i:3 * i + 3]) for i in range(len(jobs))], out[-1]
 
 
 def solution(mesh):
@@ -273,28 +281,40 @@
             parts[k] = p1, r1, p2, r2
             return s1 + s2
 
+        def job(which, k, prev):
+            p1, r1, p2, r2 = parts[k]
+            return (1, [p1] + r1, st1, prev) if which == 1 else (2, [p2] + r2, st2, prev)
+
         def step_of(k, prev, after):
-            prev, c = adam(mev, sc, *parts[k], st1, st2, prev, k, after)
+            prev, c = adam(mev, sc, n, k,
+                             [job(1, k, prev[0]), job(2, k, prev[1])], after)
             return prev, [c], gather(c)
 
-        def ahead(k, full, acc, after):
-            a = up(mev, xc, full, after)
-            return down(a, acc, full, bf if k == NK - 1 else f32)
+        def ahead(full, acc, after):
+            a = up(mev, xc, full, n, range(n), None, after)
+            return down(a, acc, full, 1, 0, f32)
 
         full = [None] * NK
         later = back(0, [])
         later = back(1, later)
         later = back(2, later)
-        prev, later, full[0] = step_of(0, None, later)
+        prev, later, full[0] = step_of(0, [None, None], later)
         prev, later, full[1] = step_of(1, prev, later)
         later = back(3, later)
         prev, later, full[2] = step_of(2, prev, later)
-        acc = ahead(0, full[0], xc, later)
-        acc = ahead(1, full[1], acc, [])
-        prev, later, full[3] = step_of(3, prev, [acc])
-        acc = ahead(2, full[2], acc, later)
-        acc = ahead(3, full[3], acc, [acc])
-        w1n, m1n, v1n, w2n, m2n, v2n = prev
+        acc = ahead(full[0], xc, later)
+        acc = ahead(full[1], acc, [])
+        acc = ahead(full[2], acc, [])
+        (n1,), c1 = adam(mev, sc, n, 3, [job(1, 3, prev[0])], [acc])
+        f1 = gather(c1)
+        half = up(mev, xc, f1[:2], n, (0, 1), None, [])
+        (n2,), c2 = adam(mev, sc, n, 3, [job(2, 3, prev[1])], [half])
+        f2 = gather(c2)
+        a = up(mev, xc, f1[2:], n, (2, 3), half, [c2])
+        acc = down(a, acc, f2[:2], 0, 0, f32)
+        acc = down(a, acc, f2[2:], 0, 1, bf)
+        w1n, m1n, v1n = n1
+        w2n, m2n, v2n = n2
         return (w1n[None], w2n[None], m1n[None], m2n[None], v1n[None], v2n[None],
                 acc.reshape(b, t, d))
 

time: 1140 us -> 1160 us (1.018)
  Pallas kernels: 510 us -> 543 us
  waiting for transfers between devices: 356 us -> 334 us
    ppermute x48 -> x51, waiting for transfers between devices: 356 us -> 334 us  [hop(): return lax.ppermute(a, 'fsdp', [(i, i ^ r) for i in range(n)])]
    pallas_call x4 -> x5, Pallas kernels: 115 us -> 134 us  [down(): pl.pallas_call(functools.partial(down_kernel, n), grid=(t // TM,), in_spe...]
    pallas_call x8 -> x10, Pallas kernels: 179 us -> 193 us  [the longest x5 124 us: up(): pl.pallas_call(functools.partial(up_kernel, n, qs), grid_spec=pltpu.Prefe...]
    ppermute x48 -> x51, starting transfers between devices: 35 us -> 35.7 us  [hop(): return lax.ppermute(a, 'fsdp', [(i, i ^ r) for i in range(n)])]
  transfers between devices with their start and end apart: 48 -> 51, of which waited for: 13 -> 14; matrix products, arithmetic and copies ran while one was open for 20% -> 20% of each run, Pallas kernels for 40% -> 44%
where the time goes in v2:
time: 1160 us; the launch traced here: 1150 us
  Pallas kernels  543 us (47%)
  waiting for transfers between devices  334 us (29%)
  matrix products  206 us (18%)
  starting transfers between devices  35.7 us (3%)
  local copies, waits for them, and re-layouts  24.7 us (2%)
    ppermute x51, waiting for transfers between devices, hop(): return lax.ppermute(a, 'fsdp', [(i, i ^ r) for i in range(n)])  334 us
    pallas_call x4, Pallas kernels, hid(): pl.pallas_call(functools.partial(hid_kernel, n), grid_spec=pltpu.Prefetch...  199 us
    pallas_call x5, Pallas kernels, down(): pl.pallas_call(functools.partial(down_kernel, n), grid=(t // TM,), in_spe...  134 us
    pallas_call x5, Pallas kernels, up(): pl.pallas_call(functools.partial(up_kernel, n, qs), grid_spec=pltpu.Prefe...  124 us
    dot_general x4, matrix products, back(): p1 = jnp.einsum('nd,nf->df', xl, dh, preferred_element_type=f32).astype(bf)  105 us
    dot_general x4, matrix products, back(): p2 = jnp.einsum('nf,nd->fd', a, gy, preferred_element_type=f32).astype(bf)  101 us
    pallas_call x5, Pallas kernels, adam(): pl.pallas_call(functools.partial(adam_kernel, n, len(jobs)), grid_spec=pl...  68.7 us
    ppermute x51, starting transfers between devices, hop(): return lax.ppermute(a, 'fsdp', [(i, i ^ r) for i in range(n)])  35.7 us
  transfers between devices with their start and end apart: 51, of which 14 were waited for; matrix products, arithmetic and copies ran while one was open for 20% of the time, Pallas kernels for 44%

profile of v2, /device:TPU:0, one launch (start us, length us, event | category | flops | bytes accessed | tf_op | source)
XLA Modules:
  0.0 1147.4 jit_solution(2476475127365730273)
XLA Ops:
  19.0 41.7 %collective-permute-done.7.refs_2_.refs_6_ = bf16[768,1536]{1,0:T(8,128)(2,1)} collective-permute-done((bf16[768,1536]{1,0:T(8,128)(2,1)}, bf16[768,1536]{1,0:T(8,128)(2,1)}, u32[]{:S(2)}, u32[]{:S(2)}) %collective-permute-start.7) | collective-permute-done | bytes 2359328 | tf_op jit(solution)/shard_map/ppermute | solution.py:247
  69.5 41.7 %collective-permute-done.4.refs_2_.refs_6_ = bf16[768,1536]{1,0:T(8,128)(2,1)} collective-permute-done((bf16[768,1536]{1,0:T(8,128)(2,1)}, bf16[768,1536]{1,0:T(8,128)(2,1)}, u32[]{:S(2)}, u32[]{:S(2)}) %collective-permute-start.4) | collective-permute-done | bytes 2359328 | tf_op jit(solution)/shard_map/ppermute | solution.py:247
  113.3 48.5 %collective-permute-done.22.refs_2_.refs_6_ = bf16[768,1536]{1,0:T(8,128)(2,1)} collective-permute-done((bf16[768,1536]{1,0:T(8,128)(2,1)}, bf16[768,1536]{1,0:T(8,128)(2,1)}, u32[]{:S(2)}, u32[]{:S(2)}) %collective-permute-start.22) | collective-permute-done | bytes 2359328 | tf_op jit(solution)/shard_map/ppermute | solution.py:247
  162.3 49.6 %hid.4 = (bf16[4096,1536]{1,0:T(8,128)(2,1)}, bf16[4096,1536]{1,0:T(8,128)(2,1)}) custom-call(s32[1]{0:T(128)} %bitcast.me, bf16[4096,1536]{1,0:T(8,128)(2,1)} %bitcast.128, bf16[4096,1536]{1,0:T(8,128)(2,1)} %bitcast.132, bf16[768,1536]{1,0:T(8,128)(2,1)} %cast_chunk.6.refs_0_.refs_4_, bf16[768,1536]{1,0:T(8,128)(2,1)} %collective-permute-done.6.refs_1_.refs_5_, ...), custom_call_target="tpu_custom_call" | custom-call | flops 38654705664 | bytes 50331648 | tf_op jit(solution)/shard_map/hid/pallas_call | solution.py:99
  211.9 26.6 %convolution_convert_fusion.7 = bf16[1536,1536]{0,1:T(8,128)(2,1)S(1)} fusion(bf16[4096,1536]{1,0:T(8,128)(2,1)} %get-tuple-element.44, bf16[1,1,4096,1536]{3,2,1,0:T(8,128)(2,1)} %param.13), kind=kOutput, calls=%fused_computation.7 | convolution fusion | flops 19329712128 | bytes 29884416 | tf_op jit(solution)/shard_map/nd,nf->df/dot_general | solution.py:276
  240.6 24.0 %convolution_convert_fusion.6.refs_4_ = bf16[1536,1536]{1,0:T(8,128)(2,1)S(1)} fusion(bf16[4096,1536]{1,0:T(8,128)(2,1)S(1)} %copy-done.35, bf16[1,4096,1536]{2,1,0:T(8,128)(2,1)} %param.14), kind=kOutput, calls=%fused_computation.6 | convolution fusion | flops 19329712128 | bytes 29884416 | tf_op jit(solution)/shard_map/nf,nd->fd/dot_general | solution.py:275
  270.7 49.7 %hid.5 = (bf16[4096,1536]{1,0:T(8,128)(2,1)}, bf16[4096,1536]{1,0:T(8,128)(2,1)}) custom-call(s32[1]{0:T(128)} %bitcast.me, bf16[4096,1536]{1,0:T(8,128)(2,1)} %bitcast.129, bf16[4096,1536]{1,0:T(8,128)(2,1)} %bitcast.133, bf16[768,1536]{1,0:T(8,128)(2,1)} %cast_chunk.5.refs_0_.refs_4_, bf16[768,1536]{1,0:T(8,128)(2,1)} %collective-permute-done.3.refs_1_.refs_5_, ...), custom_call_target="tpu_custom_call" | custom-call | flops 38654705664 | bytes 50331648 | tf_op jit(solution)/shard_map/hid/pallas_call | solution.py:99
  320.4 26.2 %convolution_convert_fusion.5 = bf16[1536,1536]{0,1:T(8,128)(2,1)S(1)} fusion(bf16[4096,1536]{1,0:T(8,128)(2,1)} %get-tuple-element.46, bf16[1,1,4096,1536]{3,2,1,0:T(8,128)(2,1)} %param.13), kind=kOutput, calls=%fused_computation.5 | convolution fusion | flops 19329712128 | bytes 29884416 | tf_op jit(solution)/shard_map/nd,nf->df/dot_general | solution.py:276
  348.6 24.0 %convolution_convert_fusion.4.refs_4_ = bf16[1536,1536]{1,0:T(8,128)(2,1)S(1)} fusion(bf16[4096,1536]{1,0:T(8,128)(2,1)S(1)} %copy-done.36, bf16[1,4096,1536]{2,1,0:T(8,128)(2,1)} %param.14), kind=kOutput, calls=%fused_computation.4 | convolution fusion | flops 19329712128 | bytes 29884416 | tf_op jit(solution)/shard_map/nf,nd->fd/dot_general | solution.py:275
  376.9 49.8 %hid.6 = (bf16[4096,1536]{1,0:T(8,128)(2,1)}, bf16[4096,1536]{1,0:T(8,128)(2,1)}) custom-call(s32[1]{0:T(128)} %bitcast.me, bf16[4096,1536]{1,0:T(8,128)(2,1)} %bitcast.130, bf16[4096,1536]{1,0:T(8,128)(2,1)} %bitcast.134, bf16[768,1536]{1,0:T(8,128)(2,1)} %cast_chunk.7.refs_0_.refs_4_, bf16[768,1536]{1,0:T(8,128)(2,1)} %collective-permute-done.21.refs_1_.refs_5_, ...), custom_call_target="tpu_custom_call" | custom-call | flops 38654705664 | bytes 50331648 | tf_op jit(solution)/shard_map/hid/pallas_call | solution.py:99
  430.8 26.3 %convolution_convert_fusion.3 = bf16[1536,1536]{0,1:T(8,128)(2,1)S(1)} fusion(bf16[4096,1536]{1,0:T(8,128)(2,1)} %get-tuple-element.48, bf16[1,1,4096,1536]{3,2,1,0:T(8,128)(2,1)} %param.13), kind=kOutput, calls=%fused_computation.3 | convolution fusion | flops 19329712128 | bytes 29884416 | tf_op jit(solution)/shard_map/nd,nf->df/dot_general | solution.py:276
  457.3 23.0 %collective-permute-done.20.refs_7_ = bf16[384,1536]{1,0:T(8,128)(2,1)S(1)} collective-permute-done((bf16[384,1536]{1,0:T(8,128)(2,1)S(1)}, bf16[384,1536]{1,0:T(8,128)(2,1)S(1)}, u32[]{:S(2)}, u32[]{:S(2)}) %collective-permute-start.20) | collective-permute-done | bytes 1179680 | tf_op jit(solution)/shard_map/ppermute | solution.py:247
  480.6 25.5 %collective-permute-done.10.refs_2_ = bf16[384,1536]{1,0:T(8,128)(2,1)S(1)} collective-permute-done((bf16[384,1536]{1,0:T(8,128)(2,1)}, bf16[384,1536]{1,0:T(8,128)(2,1)S(1)}, u32[]{:S(2)}, u32[]{:S(2)}) %collective-permute-start.10) | collective-permute-done | bytes 1179680 | tf_op jit(solution)/shard_map/ppermute | solution.py:247
  508.0 22.9 %collective-permute-done.11.refs_3_ = bf16[384,1536]{1,0:T(8,128)(2,1)S(1)} collective-permute-done((bf16[384,1536]{1,0:T(8,128)(2,1)}, bf16[384,1536]{1,0:T(8,128)(2,1)S(1)}, u32[]{:S(2)}, u32[]{:S(2)}) %collective-permute-start.11) | collective-permute-done | bytes 1179680 | tf_op jit(solution)/shard_map/ppermute | solution.py:247
  532.7 26.6 %convolution_convert_fusion.2.refs_4_ = bf16[1536,1536]{1,0:T(8,128)(2,1)S(1)} fusion(bf16[4096,1536]{1,0:T(8,128)(2,1)} %get-tuple-element.49, bf16[1,4096,1536]{2,1,0:T(8,128)(2,1)} %param.14), kind=kOutput, calls=%fused_computation.2 | convolution fusion | flops 19329712128 | bytes 29884416 | tf_op jit(solution)/shard_map/nf,nd->fd/dot_general | solution.py:275
  601.0 49.8 %hid.7 = (bf16[4096,1536]{1,0:T(8,128)(2,1)}, bf16[4096,1536]{1,0:T(8,128)(2,1)}) custom-call(s32[1]{0:T(128)} %bitcast.me, bf16[4096,1536]{1,0:T(8,128)(2,1)} %bitcast.131, bf16[4096,1536]{1,0:T(8,128)(2,1)} %bitcast.135, bf16[768,1536]{1,0:T(8,128)(2,1)} %cast_chunk.4.refs_0_.refs_4_, bf16[768,1536]{1,0:T(8,128)(2,1)} %collective-permute-done.refs_1_.refs_5_, ...), custom_call_target="tpu_custom_call" | custom-call | flops 38654705664 | bytes 50331648 | tf_op jit(solution)/shard_map/hid/pallas_call | solution.py:99
  650.7 26.2 %convolution_convert_fusion.1 = bf16[1536,1536]{0,1:T(8,128)(2,1)S(1)} fusion(bf16[4096,1536]{1,0:T(8,128)(2,1)} %get-tuple-element.58, bf16[1,1,4096,1536]{3,2,1,0:T(8,128)(2,1)} %param.13), kind=kOutput, calls=%fused_computation.1 | convolution fusion | flops 19329712128 | bytes 29884416 | tf_op jit(solution)/shard_map/nd,nf->df/dot_general | solution.py:276
  685.6 26.3 %convolution_convert_fusion.refs_0_ = bf16[1536,1536]{1,0:T(8,128)(2,1)S(1)} fusion(bf16[4096,1536]{1,0:T(8,128)(2,1)} %get-tuple-element.65, bf16[1,4096,1536]{2,1,0:T(8,128)(2,1)} %param.14), kind=kOutput, calls=%fused_computation | convolution fusion | flops 19329712128 | bytes 29884416 | tf_op jit(solution)/shard_map/nf,nd->fd/dot_general | solution.py:275
  716.9 18.3 %collective-permute-done.32.refs_7_ = bf16[384,1536]{1,0:T(8,128)(2,1)S(1)} collective-permute-done((bf16[384,1536]{1,0:T(8,128)(2,1)S(1)}, bf16[384,1536]{1,0:T(8,128)(2,1)S(1)}, u32[]{:S(2)}, u32[]{:S(2)}) %collective-permute-start.32) | collective-permute-done | bytes 1179680 | tf_op jit(solution)/shard_map/ppermute | solution.py:247
  754.7 32.1 %collective-permute-done.37.refs_2_ = bf16[768,1536]{1,0:T(8,128)(2,1)} collective-permute-done((bf16[768,1536]{1,0:T(8,128)(2,1)}, bf16[768,1536]{1,0:T(8,128)(2,1)}, u32[]{:S(2)}, u32[]{:S(2)}) %collective-permute-start.37) | collective-permute-done | bytes 2359328 | tf_op jit(solution)/shard_map/ppermute | solution.py:247
  787.3 28.5 %up.7.a = bf16[4096,1536]{1,0:T(8,128)(2,1)} custom-call(s32[1]{0:T(128)} %bitcast.me, bf16[4096,1536]{1,0:T(8,128)(2,1)} %bitcast.117, bf16[768,1536]{1,0:T(8,128)(2,1)} %get-tuple-element.56.refs_22_.refs_0_, bf16[768,1536]{1,0:T(8,128)(2,1)} %collective-permute-done.39.refs_1_, bf16[768,1536]{1,0:T(8,128)(2,1)} %collective-permute-done.40.refs_2_, ...), custom_call_target="tpu_custom_call" | custom-call | flops 19327352832 | bytes 25165824 | tf_op jit(solution)/shard_map/up/pallas_call | solution.py:141
  815.8 28.3 %down.5.acc = f32[4096,1536]{1,0:T(8,128)} custom-call(bf16[4096,1536]{1,0:T(8,128)(2,1)} %up.7.a, bf16[4096,1536]{1,0:T(8,128)(2,1)} %bitcast.118, bf16[768,1536]{1,0:T(8,128)(2,1)} %get-tuple-element.56.refs_22_.refs_0_, bf16[768,1536]{1,0:T(8,128)(2,1)} %collective-permute-done.39.refs_1_, bf16[768,1536]{1,0:T(8,128)(2,1)} %collective-permute-done.40.refs_2_, ...), custom_call_target="tpu_custom_call" | custom-call | flops 19327352832 | bytes 62914560 | tf_op jit(solution)/shard_map/down/pallas_call | solution.py:172
  846.2 28.5 %up.6.a = bf16[4096,1536]{1,0:T(8,128)(2,1)} custom-call(s32[1]{0:T(128)} %bitcast.me, bf16[4096,1536]{1,0:T(8,128)(2,1)} %bitcast.119, bf16[768,1536]{1,0:T(8,128)(2,1)} %get-tuple-element.57.refs_8_.refs_0_, bf16[768,1536]{1,0:T(8,128)(2,1)} %collective-permute-done.36.refs_1_, bf16[768,1536]{1,0:T(8,128)(2,1)} %collective-permute-done.37.refs_2_, ...), custom_call_target="tpu_custom_call" | custom-call | flops 19327352832 | bytes 25165824 | tf_op jit(solution)/shard_map/up/pallas_call | solution.py:141
  874.7 29.8 %down.6.acc = f32[4096,1536]{1,0:T(8,128)} custom-call(bf16[4096,1536]{1,0:T(8,128)(2,1)} %up.6.a, f32[4096,1536]{1,0:T(8,128)} %down.5.acc, bf16[768,1536]{1,0:T(8,128)(2,1)} %get-tuple-element.57.refs_8_.refs_0_, bf16[768,1536]{1,0:T(8,128)(2,1)} %collective-permute-done.36.refs_1_, bf16[768,1536]{1,0:T(8,128)(2,1)} %collective-permute-done.37.refs_2_, ...), custom_call_target="tpu_custom_call" | custom-call | flops 19327352832 | bytes 62914560 | tf_op jit(solution)/shard_map/down/pallas_call | solution.py:172
  904.5 28.5 %up.5.a = bf16[4096,1536]{1,0:T(8,128)(2,1)} custom-call(s32[1]{0:T(128)} %bitcast.me, bf16[4096,1536]{1,0:T(8,128)(2,1)} %bitcast.120, bf16[768,1536]{1,0:T(8,128)(2,1)} %get-tuple-element.69.refs_0_.refs_4_, bf16[768,1536]{1,0:T(8,128)(2,1)} %collective-permute-done.33.refs_1_, bf16[768,1536]{1,0:T(8,128)(2,1)} %collective-permute-done.34.refs_2_, ...), custom_call_target="tpu_custom_call" | custom-call | flops 19327352832 | bytes 25165824 | tf_op jit(solution)/shard_map/up/pallas_call | solution.py:141
  933.0 29.9 %down.7.refs_11_.acc = f32[4096,1536]{1,0:T(8,128)} custom-call(bf16[4096,1536]{1,0:T(8,128)(2,1)} %up.5.a, f32[4096,1536]{1,0:T(8,128)} %down.6.acc, bf16[768,1536]{1,0:T(8,128)(2,1)} %get-tuple-element.69.refs_0_.refs_4_, bf16[768,1536]{1,0:T(8,128)(2,1)} %collective-permute-done.33.refs_1_, bf16[768,1536]{1,0:T(8,128)(2,1)} %collective-permute-done.34.refs_2_, ...), custom_call_target="tpu_custom_call" | custom-call | flops 19327352832 | bytes 62914560 | tf_op jit(solution)/shard_map/down/pallas_call | solution.py:172
  976.3 16.4 %up.8.refs_11_.refs_2_ = f32[4096,1536]{1,0:T(8,128)} custom-call(s32[1]{0:T(128)} %bitcast.me, bf16[4096,1536]{1,0:T(8,128)(2,1)} %bitcast.121, bf16[384,1536]{1,0:T(8,128)(2,1)} %get-tuple-element.74.refs_0_, bf16[384,1536]{1,0:T(8,128)(2,1)} %collective-permute-done.45.refs_1_), custom_call_target="tpu_custom_call" | custom-call | flops 9663676416 | bytes 25165824 | tf_op jit(solution)/shard_map/up/pallas_call | solution.py:141
  1002.3 24.2 %collective-permute-done.44.refs_3_ = bf16[384,1536]{1,0:T(8,128)(2,1)} collective-permute-done((bf16[384,1536]{1,0:T(8,128)(2,1)S(1)}, bf16[384,1536]{1,0:T(8,128)(2,1)}, u32[]{:S(2)}, u32[]{:S(2)}) %collective-permute-start.44) | collective-permute-done | bytes 1179680 | tf_op jit(solution)/shard_map/ppermute | solution.py:247
  1053.4 23.7 %collective-permute-done.49.refs_0_ = bf16[384,1536]{1,0:T(8,128)(2,1)S(1)} collective-permute-done((bf16[384,1536]{1,0:T(8,128)(2,1)}, bf16[384,1536]{1,0:T(8,128)(2,1)S(1)}, u32[]{:S(2)}, u32[]{:S(2)}) %collective-permute-start.49) | collective-permute-done | bytes 1179680 | tf_op jit(solution)/shard_map/ppermute | solution.py:247
  1078.2 22.2 %up.9.a = bf16[4096,1536]{1,0:T(8,128)(2,1)} custom-call(s32[1]{0:T(128)} %bitcast.me, bf16[4096,1536]{1,0:T(8,128)(2,1)} %bitcast.122, bf16[384,1536]{1,0:T(8,128)(2,1)} %collective-permute-done.46.refs_0_, bf16[384,1536]{1,0:T(8,128)(2,1)} %copy-done.22, f32[4096,1536]{1,0:T(8,128)} %up.8.refs_11_.refs_2_, bf16[384,1536]{1,0:T(8,128)(2,1)} %get-tuple-element.80.refs_3_.refs_0_), custom_call_target="tpu_custom_call" | custom-call | flops 9663676416 | bytes 25165824 | tf_op jit(solution)/shard_map/up/pallas_call | solution.py:141
  1100.4 24.8 %down.8.acc = f32[4096,1536]{1,0:T(8,128)} custom-call(bf16[4096,1536]{1,0:T(8,128)(2,1)} %up.9.a, f32[4096,1536]{1,0:T(8,128)} %down.7.refs_11_.acc, bf16[384,1536]{1,0:T(8,128)(2,1)} %get-tuple-element.80.refs_3_.refs_0_, bf16[384,1536]{1,0:T(8,128)(2,1)} %collective-permute-done.48.refs_1_), custom_call_target="tpu_custom_call" | custom-call | flops 9663676416 | bytes 62914560 | tf_op jit(solution)/shard_map/down/pallas_call | solution.py:172
  1126.3 20.9 %down.9 = bf16[4096,1536]{1,0:T(8,128)(2,1)} custom-call(bf16[4096,1536]{1,0:T(8,128)(2,1)} %up.9.a, f32[4096,1536]{1,0:T(8,128)} %down.8.acc, bf16[384,1536]{1,0:T(8,128)(2,1)} %copy-done.20, bf16[384,1536]{1,0:T(8,128)(2,1)} %copy-done.21), custom_call_target="tpu_custom_call" | custom-call | flops 9663676416 | bytes 62914560 | tf_op jit(solution)/shard_map/down/pallas_call | solution.py:172
  (185 shorter events, 179.8 us)
Async XLA Ops:
  8.3 61.3 %collective-permute-start.6 = (bf16[768,1536]{1,0:T(8,128)(2,1)}, bf16[768,1536]{1,0:T(8,128)(2,1)}, u32[]{:S(2)}, u32[]{:S(2)}) collective-permute-start(bf16[768,1536]{1,0:T(8,128)(2,1)} %cast_chunk.6.refs_0_.refs_4_), channel_id=1, source_target_pairs={{0,1},{1,0},{2,3},{3,2},{4,5},{5,4},{6,7},{7,6}} | collective-permute-start | bytes 7077896 | tf_op jit(solution)/shard_map/ppermute | solution.py:247
  12.6 98.6 %collective-permute-start.4 = (bf16[768,1536]{1,0:T(8,128)(2,1)}, bf16[768,1536]{1,0:T(8,128)(2,1)}, u32[]{:S(2)}, u32[]{:S(2)}) collective-permute-start(bf16[768,1536]{1,0:T(8,128)(2,1)} %cast_chunk.5.refs_0_.refs_4_), channel_id=1, source_target_pairs={{0,2},{1,3},{2,0},{3,1},{4,6},{5,7},{6,4},{7,5}} | collective-permute-start | bytes 7077896 | tf_op jit(solution)/shard_map/ppermute | solution.py:247
  17.1 144.7 %collective-permute-start.22 = (bf16[768,1536]{1,0:T(8,128)(2,1)}, bf16[768,1536]{1,0:T(8,128)(2,1)}, u32[]{:S(2)}, u32[]{:S(2)}) collective-permute-start(bf16[768,1536]{1,0:T(8,128)(2,1)} %cast_chunk.7.refs_0_.refs_4_), channel_id=1, source_target_pairs={{0,2},{1,3},{2,0},{3,1},{4,6},{5,7},{6,4},{7,5}} | collective-permute-start | bytes 7077896 | tf_op jit(solution)/shard_map/ppermute | solution.py:247
  60.7 101.1 %collective-permute-start.8 = (bf16[768,1536]{1,0:T(8,128)(2,1)}, bf16[768,1536]{1,0:T(8,128)(2,1)}, u32[]{:S(2)}, u32[]{:S(2)}) collective-permute-start(bf16[768,1536]{1,0:T(8,128)(2,1)} %collective-permute-done.7.refs_2_.refs_6_), channel_id=1, source_target_pairs={{0,1},{1,0},{2,3},{3,2},{4,5},{5,4},{6,7},{7,6}} | collective-permute-start | bytes 7077896 | tf_op jit(solution)/shard_map/ppermute | solution.py:247
  60.7 208.0 %collective-permute-start.3 = (bf16[768,1536]{1,0:T(8,128)(2,1)S(1)}, bf16[768,1536]{1,0:T(8,128)(2,1)}, u32[]{:S(2)}, u32[]{:S(2)}) collective-permute-start(bf16[768,1536]{1,0:T(8,128)(2,1)S(1)} %copy-done.19), channel_id=1, source_target_pairs={{0,1},{1,0},{2,3},{3,2},{4,5},{5,4},{6,7},{7,6}} | collective-permute-start | bytes 7077896 | tf_op jit(solution)/shard_map/ppermute | solution.py:247
  69.5 307.1 %collective-permute-start.21 = (bf16[768,1536]{1,0:T(8,128)(2,1)}, bf16[768,1536]{1,0:T(8,128)(2,1)}, u32[]{:S(2)}, u32[]{:S(2)}) collective-permute-start(bf16[768,1536]{1,0:T(8,128)(2,1)} %cast_chunk.7.refs_0_.refs_4_), channel_id=1, source_target_pairs={{0,1},{1,0},{2,3},{3,2},{4,5},{5,4},{6,7},{7,6}} | collective-permute-start | bytes 7077896 | tf_op jit(solution)/shard_map/ppermute | solution.py:247
  111.2 315.4 %collective-permute-start.1 = (bf16[768,1536]{1,0:T(8,128)(2,1)}, bf16[768,1536]{1,0:T(8,128)(2,1)}, u32[]{:S(2)}, u32[]{:S(2)}) collective-permute-start(bf16[768,1536]{1,0:T(8,128)(2,1)} %cast_chunk.4.refs_0_.refs_4_), channel_id=1, source_target_pairs={{0,2},{1,3},{2,0},{3,1},{4,6},{5,7},{6,4},{7,5}} | collective-permute-start | bytes 7077896 | tf_op jit(solution)/shard_map/ppermute | solution.py:247
  161.8 106.9 %collective-permute-start.5 = (bf16[768,1536]{1,0:T(8,128)(2,1)}, bf16[768,1536]{1,0:T(8,128)(2,1)}, u32[]{:S(2)}, u32[]{:S(2)}) collective-permute-start(bf16[768,1536]{1,0:T(8,128)(2,1)} %collective-permute-done.4.refs_2_.refs_6_), channel_id=1, source_target_pairs={{0,1},{1,0},{2,3},{3,2},{4,5},{5,4},{6,7},{7,6}} | collective-permute-start | bytes 7077896 | tf_op jit(solution)/shard_map/ppermute | solution.py:247
  161.8 214.9 %collective-permute-start.23 = (bf16[768,1536]{1,0:T(8,128)(2,1)}, bf16[768,1536]{1,0:T(8,128)(2,1)}, u32[]{:S(2)}, u32[]{:S(2)}) collective-permute-start(bf16[768,1536]{1,0:T(8,128)(2,1)} %collective-permute-done.22.refs_2_.refs_6_), channel_id=1, source_target_pairs={{0,1},{1,0},{2,3},{3,2},{4,5},{5,4},{6,7},{7,6}} | collective-permute-start | bytes 7077896 | tf_op jit(solution)/shard_map/ppermute | solution.py:247
  268.7 159.9 %collective-permute-start.15 = (bf16[384,1536]{1,0:T(8,128)(2,1)}, bf16[384,1536]{1,0:T(8,128)(2,1)}, u32[]{:S(2)}, u32[]{:S(2)}) collective-permute-start(bf16[384,1536]{1,0:T(8,128)(2,1)} %get-tuple-element.104.refs_8_), channel_id=1, source_target_pairs={{0,1},{1,0},{2,3},{3,2},{4,5},{5,4},{6,7},{7,6}} | collective-permute-start | bytes 3538952 | tf_op jit(solution)/shard_map/ppermute | solution.py:247
  268.7 159.9 %collective-permute-start.16 = (bf16[384,1536]{1,0:T(8,128)(2,1)}, bf16[384,1536]{1,0:T(8,128)(2,1)}, u32[]{:S(2)}, u32[]{:S(2)}) collective-permute-start(bf16[384,1536]{1,0:T(8,128)(2,1)} %get-tuple-element.103.refs_9_), channel_id=1, source_target_pairs={{0,2},{1,3},{2,0},{3,1},{4,6},{5,7},{6,4},{7,5}} | collective-permute-start | bytes 3538952 | tf_op jit(solution)/shard_map/ppermute | solution.py:247
  428.6 77.5 %collective-permute-start.10 = (bf16[384,1536]{1,0:T(8,128)(2,1)}, bf16[384,1536]{1,0:T(8,128)(2,1)S(1)}, u32[]{:S(2)}, u32[]{:S(2)}) collective-permute-start(bf16[384,1536]{1,0:T(8,128)(2,1)} %get-tuple-element.97.refs_9_), channel_id=1, source_target_pairs={{0,2},{1,3},{2,0},{3,1},{4,6},{5,7},{6,4},{7,5}} | collective-permute-start | bytes 3538952 | tf_op jit(solution)/shard_map/ppermute | solution.py:247
  430.2 100.7 %collective-permute-start.11 = (bf16[384,1536]{1,0:T(8,128)(2,1)}, bf16[384,1536]{1,0:T(8,128)(2,1)S(1)}, u32[]{:S(2)}, u32[]{:S(2)}) collective-permute-start(bf16[384,1536]{1,0:T(8,128)(2,1)} %get-tuple-element.96.refs_10_), channel_id=1, source_target_pairs={{0,3},{1,2},{2,1},{3,0},{4,7},{5,6},{6,5},{7,4}} | collective-permute-start | bytes 3538952 | tf_op jit(solution)/shard_map/ppermute | solution.py:247
  430.4 102.3 %collective-permute-start.12 = (bf16[384,1536]{1,0:T(8,128)(2,1)}, bf16[384,1536]{1,0:T(8,128)(2,1)S(1)}, u32[]{:S(2)}, u32[]{:S(2)}) collective-permute-start(bf16[384,1536]{1,0:T(8,128)(2,1)} %get-tuple-element.95.refs_11_), channel_id=1, source_target_pairs={{0,1},{1,0},{2,3},{3,2},{4,5},{5,4},{6,7},{7,6}} | collective-permute-start | bytes 3538952 | tf_op jit(solution)/shard_map/ppermute | solution.py:247
  457.1 141.9 %collective-permute-start = (bf16[768,1536]{1,0:T(8,128)(2,1)}, bf16[768,1536]{1,0:T(8,128)(2,1)}, u32[]{:S(2)}, u32[]{:S(2)}) collective-permute-start(bf16[768,1536]{1,0:T(8,128)(2,1)} %cast_chunk.4.refs_0_.refs_4_), channel_id=1, source_target_pairs={{0,1},{1,0},{2,3},{3,2},{4,5},{5,4},{6,7},{7,6}} | collective-permute-start | bytes 7077896 | tf_op jit(solution)/shard_map/ppermute | solution.py:247
  480.2 119.2 %collective-permute-start.2 = (bf16[768,1536]{1,0:T(8,128)(2,1)}, bf16[768,1536]{1,0:T(8,128)(2,1)}, u32[]{:S(2)}, u32[]{:S(2)}) collective-permute-start(bf16[768,1536]{1,0:T(8,128)(2,1)} %collective-permute-done.1.refs_2_.refs_6_), channel_id=1, source_target_pairs={{0,1},{1,0},{2,3},{3,2},{4,5},{5,4},{6,7},{7,6}} | collective-permute-start | bytes 7077896 | tf_op jit(solution)/shard_map/ppermute | solution.py:247
  506.1 74.0 %collective-permute-start.13 = (bf16[384,1536]{1,0:T(8,128)(2,1)}, bf16[384,1536]{1,0:T(8,128)(2,1)}, u32[]{:S(2)}, u32[]{:S(2)}) collective-permute-start(bf16[384,1536]{1,0:T(8,128)(2,1)} %get-tuple-element.94.refs_12_), channel_id=1, source_target_pairs={{0,2},{1,3},{2,0},{3,1},{4,6},{5,7},{6,4},{7,5}} | collective-permute-start | bytes 3538952 | tf_op jit(solution)/shard_map/ppermute | solution.py:247
  580.1 96.8 %collective-permute-start.27 = (bf16[384,1536]{1,0:T(8,128)(2,1)}, bf16[384,1536]{1,0:T(8,128)(2,1)}, u32[]{:S(2)}, u32[]{:S(2)}) collective-permute-start(bf16[384,1536]{1,0:T(8,128)(2,1)} %get-tuple-element.92.refs_16_), channel_id=1, source_target_pairs={{0,1},{1,0},{2,3},{3,2},{4,5},{5,4},{6,7},{7,6}} | collective-permute-start | bytes 3538952 | tf_op jit(solution)/shard_map/ppermute | solution.py:247
  580.9 96.6 %collective-permute-start.28 = (bf16[384,1536]{1,0:T(8,128)(2,1)S(1)}, bf16[384,1536]{1,0:T(8,128)(2,1)}, u32[]{:S(2)}, u32[]{:S(2)}) collective-permute-start(bf16[384,1536]{1,0:T(8,128)(2,1)S(1)} %copy-done.12), channel_id=1, source_target_pairs={{0,2},{1,3},{2,0},{3,1},{4,6},{5,7},{6,4},{7,5}} | collective-permute-start | bytes 3538952 | tf_op jit(solution)/shard_map/ppermute | solution.py:247
  582.4 96.0 %collective-permute-start.29 = (bf16[384,1536]{1,0:T(8,128)(2,1)S(1)}, bf16[384,1536]{1,0:T(8,128)(2,1)}, u32[]{:S(2)}, u32[]{:S(2)}) collective-permute-start(bf16[384,1536]{1,0:T(8,128)(2,1)S(1)} %copy-done.11), channel_id=1, source_target_pairs={{0,3},{1,2},{2,1},{3,0},{4,7},{5,6},{6,5},{7,4}} | collective-permute-start | bytes 3538952 | tf_op jit(solution)/shard_map/ppermute | solution.py:247
  599.0 80.1 %collective-permute-start.30 = (bf16[384,1536]{1,0:T(8,128)(2,1)S(1)}, bf16[384,1536]{1,0:T(8,128)(2,1)}, u32[]{:S(2)}, u32[]{:S(2)}) collective-permute-start(bf16[384,1536]{1,0:T(8,128)(2,1)S(1)} %copy-done.10), channel_id=1, source_target_pairs={{0,1},{1,0},{2,3},{3,2},{4,5},{5,4},{6,7},{7,6}} | collective-permute-start | bytes 3538952 | tf_op jit(solution)/shard_map/ppermute | solution.py:247
  599.4 86.3 %collective-permute-start.40 = (bf16[768,1536]{1,0:T(8,128)(2,1)}, bf16[768,1536]{1,0:T(8,128)(2,1)}, u32[]{:S(2)}, u32[]{:S(2)}) collective-permute-start(bf16[768,1536]{1,0:T(8,128)(2,1)} %get-tuple-element.56.refs_22_.refs_0_), channel_id=1, source_target_pairs={{0,2},{1,3},{2,0},{3,1},{4,6},{5,7},{6,4},{7,5}} | collective-permute-start | bytes 7077896 | tf_op jit(solution)/shard_map/ppermute | solution.py:247
  678.4 76.0 %collective-permute-start.39 = (bf16[768,1536]{1,0:T(8,128)(2,1)}, bf16[768,1536]{1,0:T(8,128)(2,1)}, u32[]{:S(2)}, u32[]{:S(2)}) collective-permute-start(bf16[768,1536]{1,0:T(8,128)(2,1)} %get-tuple-element.56.refs_22_.refs_0_), channel_id=1, source_target_pairs={{0,1},{1,0},{2,3},{3,2},{4,5},{5,4},{6,7},{7,6}} | collective-permute-start | bytes 7077896 | tf_op jit(solution)/shard_map/ppermute | solution.py:247
  679.1 107.6 %collective-permute-start.37 = (bf16[768,1536]{1,0:T(8,128)(2,1)}, bf16[768,1536]{1,0:T(8,128)(2,1)}, u32[]{:S(2)}, u32[]{:S(2)}) collective-permute-start(bf16[768,1536]{1,0:T(8,128)(2,1)} %get-tuple-element.57.refs_8_.refs_0_), channel_id=1, source_target_pairs={{0,2},{1,3},{2,0},{3,1},{4,6},{5,7},{6,4},{7,5}} | collective-permute-start | bytes 7077896 | tf_op jit(solution)/shard_map/ppermute | solution.py:247
  685.6 101.1 %collective-permute-start.41 = (bf16[768,1536]{1,0:T(8,128)(2,1)}, bf16[768,1536]{1,0:T(8,128)(2,1)}, u32[]{:S(2)}, u32[]{:S(2)}) collective-permute-start(bf16[768,1536]{1,0:T(8,128)(2,1)} %collective-permute-done.40.refs_2_), channel_id=1, source_target_pairs={{0,1},{1,0},{2,3},{3,2},{4,5},{5,4},{6,7},{7,6}} | collective-permute-start | bytes 7077896 | tf_op jit(solution)/shard_map/ppermute | solution.py:247
  716.4 127.7 %collective-permute-start.36 = (bf16[768,1536]{1,0:T(8,128)(2,1)}, bf16[768,1536]{1,0:T(8,128)(2,1)}, u32[]{:S(2)}, u32[]{:S(2)}) collective-permute-start(bf16[768,1536]{1,0:T(8,128)(2,1)} %get-tuple-element.57.refs_8_.refs_0_), channel_id=1, source_target_pairs={{0,1},{1,0},{2,3},{3,2},{4,5},{5,4},{6,7},{7,6}} | collective-permute-start | bytes 7077896 | tf_op jit(solution)/shard_map/ppermute | solution.py:247
  752.6 93.0 %collective-permute-start.34 = (bf16[768,1536]{1,0:T(8,128)(2,1)}, bf16[768,1536]{1,0:T(8,128)(2,1)}, u32[]{:S(2)}, u32[]{:S(2)}) collective-permute-start(bf16[768,1536]{1,0:T(8,128)(2,1)} %get-tuple-element.69.refs_0_.refs_4_), channel_id=1, source_target_pairs={{0,2},{1,3},{2,0},{3,1},{4,6},{5,7},{6,4},{7,5}} | collective-permute-start | bytes 7077896 | tf_op jit(solution)/shard_map/ppermute | solution.py:247
  754.3 150.1 %collective-permute-start.33 = (bf16[768,1536]{1,0:T(8,128)(2,1)}, bf16[768,1536]{1,0:T(8,128)(2,1)}, u32[]{:S(2)}, u32[]{:S(2)}) collective-permute-start(bf16[768,1536]{1,0:T(8,128)(2,1)} %get-tuple-element.69.refs_0_.refs_4_), channel_id=1, source_target_pairs={{0,1},{1,0},{2,3},{3,2},{4,5},{5,4},{6,7},{7,6}} | collective-permute-start | bytes 7077896 | tf_op jit(solution)/shard_map/ppermute | solution.py:247
  786.8 176.0 %collective-permute-start.24 = (bf16[384,1536]{1,0:T(8,128)(2,1)S(1)}, bf16[384,1536]{1,0:T(8,128)(2,1)}, u32[]{:S(2)}, u32[]{:S(2)}) collective-permute-start(bf16[384,1536]{1,0:T(8,128)(2,1)S(1)} %copy-done.18), channel_id=1, source_target_pairs={{0,1},{1,0},{2,3},{3,2},{4,5},{5,4},{6,7},{7,6}} | collective-permute-start | bytes 3538952 | tf_op jit(solution)/shard_map/ppermute | solution.py:247
  844.0 118.8 %collective-permute-start.25 = (bf16[384,1536]{1,0:T(8,128)(2,1)S(1)}, bf16[384,1536]{1,0:T(8,128)(2,1)}, u32[]{:S(2)}, u32[]{:S(2)}) collective-permute-start(bf16[384,1536]{1,0:T(8,128)(2,1)S(1)} %copy-done.17), channel_id=1, source_target_pairs={{0,2},{1,3},{2,0},{3,1},{4,6},{5,7},{6,4},{7,5}} | collective-permute-start | bytes 3538952 | tf_op jit(solution)/shard_map/ppermute | solution.py:247
  845.6 117.2 %collective-permute-start.26 = (bf16[384,1536]{1,0:T(8,128)(2,1)S(1)}, bf16[384,1536]{1,0:T(8,128)(2,1)}, u32[]{:S(2)}, u32[]{:S(2)}) collective-permute-start(bf16[384,1536]{1,0:T(8,128)(2,1)S(1)} %copy-done.16), channel_id=1, source_target_pairs={{0,3},{1,2},{2,1},{3,0},{4,7},{5,6},{6,5},{7,4}} | collective-permute-start | bytes 3538952 | tf_op jit(solution)/shard_map/ppermute | solution.py:247
  974.9 78.0 %collective-permute-start.46 = (bf16[384,1536]{1,0:T(8,128)(2,1)}, bf16[384,1536]{1,0:T(8,128)(2,1)}, u32[]{:S(2)}, u32[]{:S(2)}) collective-permute-start(bf16[384,1536]{1,0:T(8,128)(2,1)} %get-tuple-element.74.refs_0_), channel_id=1, source_target_pairs={{0,2},{1,3},{2,0},{3,1},{4,6},{5,7},{6,4},{7,5}} | collective-permute-start | bytes 3538952 | tf_op jit(solution)/shard_map/ppermute | solution.py:247
  (56 other events, 1965.3 us)
